TPU v7x, 8 devices: a whole 2x2x1 slice. The times are simulated.
8 devices in a mesh: dp: 1 (over z), col: 2 (over y), row: 4 (over x, core).
Axes of the slice: x: 2, y: 2, z: 1, core: 2. Of those that a mesh axis runs over, the one named last changes fastest.
Arguments:
- act_in: bfloat16 [8192, 16384], P(('dp', 'row'), 'col')
- w_down: bfloat16 [16384, 4096], P('row', 'col')
- grad_out: bfloat16 [8192, 4096], P(('dp', 'row'), 'col')
Outputs:
- output 1: bfloat16 [8192, 16384], P(('dp', 'row'), 'col')
- output 2: float32 [16384, 4096], P(('dp', 'row'), 'col')
All inputs are finite; a program needn't handle non-finite values.
Results may differ from a plain program's by a relative error of at most 0.001.
Values are sent between devices in bfloat16 or wider.
A program may use at most 1 GiB of HBM per device.

v0:
```python
import jax
import jax.numpy as jnp
from jax import lax
from jax.sharding import PartitionSpec as P


def solution(mesh):
    io_spec = P(("dp", "row"), "col")
    w_spec = P("row", "col")

    def local_backward(act_blk, w_blk, grad_blk):
        w_cols = lax.all_gather(w_blk, "row", axis=0, tiled=True)
        grad_in_part = jnp.einsum("tn,kn->tk", grad_blk, w_cols, preferred_element_type=jnp.float32)
        grad_in = lax.psum_scatter(grad_in_part, "col", scatter_dimension=1, tiled=True).astype(jnp.bfloat16)
        act_rows = lax.all_gather(act_blk, "col", axis=1, tiled=True)
        grad_w_part = jnp.einsum("tk,tn->kn", act_rows, grad_blk, preferred_element_type=jnp.float32)
        grad_w = lax.psum_scatter(grad_w_part, "row", scatter_dimension=0, tiled=True)
        return grad_in, grad_w

    return jax.shard_map(local_backward, mesh=mesh, in_specs=(io_spec, w_spec, io_spec), out_specs=(io_spec, io_spec), check_vma=False)
```

profile of v0, /device:TPU:0, one launch (start us, length us, event | category | flops | bytes accessed | tf_op | source)
XLA Modules:
  0.0 3492.9 jit_solution(11051449493008785920)
XLA Ops:
  7.2 0.0 all-gather.3.cloned.1.call-start
  7.2 0.7 all-gather.3.cloned.1.call-update
  7.9 0.0 all-gather.5.cloned.1.call-start
  7.9 0.7 all-gather.5.cloned.1.call-update
  8.6 0.0 reduce-scatter.5.cloned.1.call-start
  8.7 393.3 %all-gather.3.cloned.1.call-done = bf16[16384,2048]{1,0:T(8,128)(2,1)} async-done(((bf16[4096,2048]{1,0:T(8,128)(2,1)}), bf16[16384,2048]{1,0:T(8,128)(2,1)}) %all-gather.3.cloned.1.call-update) | async-done | bytes 67108880 | tf_op jit(solution)/shard_map/all_gather | solution.py:12
  402.0 150.9 %fusion = f32[2048,16384]{1,0:T(8,128)} fusion(bf16[2048,2048]{1,0:T(8,128)(2,1)} %param.5, bf16[16384,2048]{1,0:T(8,128)(2,1)} %all-gather.3.cloned.1.call-done), kind=kOutput, calls=%fused_computation | convolution fusion | flops 137438953472 | bytes 209715200 | tf_op jit(solution)/shard_map/tn,kn->tk/dot_general | solution.py:13
  552.9 0.0 reduce-scatter.5.cloned.1.call-update
  553.0 0.0 reduce-scatter.7.cloned.1.call-start
  553.0 613.7 %all-gather.5.cloned.1.call-done = bf16[2048,16384]{1,0:T(8,128)(2,1)} async-done(((bf16[2048,8192]{1,0:T(8,128)(2,1)}), bf16[2048,16384]{1,0:T(8,128)(2,1)}) %all-gather.5.cloned.1.call-update) | async-done | bytes 67108880 | tf_op jit(solution)/shard_map/all_gather | solution.py:15
  1166.8 153.5 %fusion.1 = f32[16384,2048]{1,0:T(8,128)} fusion(bf16[2048,16384]{1,0:T(8,128)(2,1)} %all-gather.5.cloned.1.call-done, bf16[2048,2048]{1,0:T(8,128)(2,1)} %param.5), kind=kOutput, calls=%fused_computation.1 | convolution fusion | flops 137438953472 | bytes 209715200 | tf_op jit(solution)/shard_map/tk,tn->kn/dot_general | solution.py:16
  1320.3 0.0 reduce-scatter.7.cloned.1.call-update
  1320.3 1293.5 %reduce-scatter.5.cloned.1.call-done = f32[2048,8192]{1,0:T(8,128)} async-done(((f32[2048,16384]{1,0:T(8,128)}), f32[2048,8192]{1,0:T(8,128)}) %reduce-scatter.5.cloned.1.call-update) | async-done | bytes 67108880 | tf_op jit(solution)/shard_map/reduce_scatter | solution.py:14
  2613.7 32.3 convert_element_type.3
  2646.1 840.3 %reduce-scatter.7.cloned.1.call-done = f32[4096,2048]{1,0:T(8,128)} async-done(((f32[16384,2048]{1,0:T(8,128)}), f32[4096,2048]{1,0:T(8,128)}) %reduce-scatter.7.cloned.1.call-update) | async-done | bytes 33554448
Async XLA Ops:
  7.2 394.9 %all-gather.3.cloned.1.call-start = ((), (), s32[]{:S(2)}) async-start(), calls=%async_computation.2 | async-start | bytes 83886080 | tf_op jit(solution)/shard_map/all_gather | solution.py:12
  7.9 1158.9 %all-gather.5.cloned.1.call-start = ((), (), s32[]{:S(2)}) async-start(), calls=%async_computation.4 | async-start | bytes 100663296 | tf_op jit(solution)/shard_map/all_gather | solution.py:15
  8.6 2605.1 %reduce-scatter.5.cloned.1.call-start = ((), (), s32[]{:S(2)}) async-start(), calls=%async_computation.3 | async-start | bytes 201326592 | tf_op jit(solution)/shard_map/reduce_scatter | solution.py:14
  553.0 2933.4 %reduce-scatter.7.cloned.1.call-start = ((), (), s32[]{:S(2)}) async-start(), calls=%async_computation.5 | async-start | bytes 167772160
Sparse Core Ops, SparseCore 0:
  9.5 392.4 all-gather.2
  403.6 763.1 all-gather.4
  1169.0 1444.6 reduce-scatter.4
  2616.7 869.6 reduce-scatter.6
where the time goes:
time: 3490 us
  waiting for transfers between devices  3140 us (90%)
  matrix products  304 us (9%)
    reduce_scatter x1, waiting for transfers between devices, local_backward(): lax.psum_scatter(grad_in_part, 'col', scatter_dimension=1, tiled=True)  1290 us
    unnamed x5, waiting for transfers between devices  842 us
    all_gather x1, waiting for transfers between devices, local_backward(): act_rows = lax.all_gather(act_blk, 'col', axis=1, tiled=True)  614 us
    all_gather x1, waiting for transfers between devices, local_backward(): w_cols = lax.all_gather(w_blk, 'row', axis=0, tiled=True)  393 us
    dot_general x1, matrix products, local_backward(): jnp.einsum('tk,tn->kn', act_rows, grad_blk, preferred_element_type=jnp.fl...  154 us
    dot_general x1, matrix products, local_backward(): jnp.einsum('tn,kn->tk', grad_blk, w_cols, preferred_element_type=jnp.floa...  151 us
  transfers between devices with their start and end apart: 4, of which 4 were waited for; matrix products, arithmetic and copies ran while one was open for 10% of the time, Pallas kernels for 0%

commit v1 on v0

v1 whole, which is shorter than its diff:
```python
import jax
import jax.numpy as jnp
from jax import lax
from jax.sharding import PartitionSpec as P


CHUNKS = 8
AHEAD = 6
AXES = ("col", "row")
W_ORDER = ("o0", "o1", "o2", "o3", "o4", "o5", "y0", "o6", "y1", "o7", "y2", "y3", "y4", "y5", "y6", "y7")


def _dev(x, y, q):
    return y * 4 + x * 2 + q


def _chips():
    return [(x, y, q) for x in (0, 1) for y in (0, 1) for q in (0, 1)]


Y_SWAP = [(_dev(x, y, q), _dev(x, 1 - y, q)) for x, y, q in _chips()]
X_SWAP = [(_dev(x, y, q), _dev(1 - x, y, q)) for x, y, q in _chips()]
X_CROSS = [(_dev(x, y, q), _dev(1 - x, y, q if x == y else 1 - q)) for x, y, q in _chips()]
Q_SWAP = [(_dev(x, y, q), _dev(x, y, 1 - q)) for x, y, q in _chips()]
Y_TO_DIAG = [pair for pair, (x, y, q) in zip(Y_SWAP, _chips()) if x != y]
Y_FROM_DIAG = [pair for pair, (x, y, q) in zip(Y_SWAP, _chips()) if x == y]


def _send(value, pairs):
    return lax.ppermute(value, AXES, pairs)


def _tie(value, *deps):
    deps = tuple(d for d in deps if d is not None)
    if not deps:
        return value
    return lax.optimization_barrier((value,) + deps)[0]


def _tdot(a, b):
    return lax.dot_general(a, b, (((0,), (0,)), ((), ())), preferred_element_type=jnp.float32)


def _dot(a, b):
    return lax.dot_general(a, b, (((1,), (0,)), ((), ())), preferred_element_type=jnp.float32)


def solution(mesh):
    io_spec = P(("dp", "row"), "col")
    w_spec = P("row", "col")

    def local_backward(act_blk, w_blk, grad_blk):
        row = lax.axis_index("row")
        col = lax.axis_index("col")
        core = row % 2
        diag = (row // 2) == col
        tokens, wide = act_blk.shape
        feats, outs = w_blk.shape
        half = outs // 2
        width = feats // CHUNKS

        def cut(a, j):
            return a[:, j * width : (j + 1) * width]

        g_y, g_x, g_d = [None] * 2, [None] * 2, [None] * 2
        piece = [grad_blk[:, :half], grad_blk[:, half:]]
        g_x[0] = _send(piece[0], X_SWAP)
        g_y[0] = _send(piece[0], Y_SWAP)
        g_d[0] = _send(g_x[0], Y_TO_DIAG)

        w_t = w_blk.T
        x_same = lax.dynamic_slice(act_blk, (0, core * feats), (tokens, feats))
        x_other = lax.dynamic_slice(act_blk, (0, (1 - core) * feats), (tokens, feats))

        g_q = _send(grad_blk, Q_SWAP)
        x_q = [_send(cut(x_other, j), Q_SWAP) for j in range(CHUNKS)]

        g_y[1] = _send(piece[1], Y_SWAP)

        g_x[1] = _send(piece[1], X_SWAP)
        g_d[1] = _send(g_x[1], Y_TO_DIAG)
        w_y = [_send(_tie(cut(w_t, j), g_d[0]), Y_TO_DIAG) for j in range(CHUNKS)]
        got, got_w = [], {}

        def exchange(p, dep=None):
            name = W_ORDER[p]
            j = int(name[1:])
            w_part = cut(w_t, j) if name[0] == "o" else w_y[j]
            x_part = cut(x_same if p % 2 == 0 else x_other, p // 2)
            if name[0] == "o":
                load = _tie(jnp.where(diag, w_part, x_part), dep)
            else:
                load = jnp.where(diag, w_part, _tie(x_part, dep))
            got.append(_send(load, X_SWAP if p % 2 == 0 else X_CROSS))
            got_w[name] = (w_part, got[-1], p)

        for p in range(AHEAD):
            exchange(p)

        g_yq = [_send(g, Q_SWAP) for g in g_y]
        g_xq = [_send(g, Q_SWAP) for g in g_x]
        g_dq = [_send(g, Q_SWAP) for g in g_d]
        g_yc = jnp.concatenate(g_y, axis=1)
        g_xc = jnp.concatenate(g_x, axis=1)
        g_xqc = jnp.concatenate(g_xq, axis=1)

        grad_in = jnp.zeros((tokens, wide), jnp.bfloat16)
        grad_w = jnp.zeros((feats, outs), jnp.float32)
        ready = {}
        last = None
        for step in range(CHUNKS):
            r1, r2 = got[2 * step], got[2 * step + 1]
            x_a, x_b = cut(x_same, step), x_q[step]
            r1, r2 = _tie(r1, last), _tie(r2, last)
            sent = []
            prev = None
            for h in range(2):
                local = _tdot(x_a, g_y[h]) + _tdot(x_b, g_yq[h])
                far = local + _tdot(_tie(r1, prev), g_d[h]) + _tdot(r2, g_dq[h])
                sent.append(_send(far, Y_FROM_DIAG))
                prev = far
            if step > 0:
                while len(got) < min(2 * step + AHEAD, 2 * CHUNKS):
                    exchange(len(got), prev)
            near = _tdot(x_a, grad_blk) + _tdot(x_b, g_q)
            near = near + _tdot(_tie(r1, prev), g_xc) + _tdot(r2, g_xqc)
            last = near
            for h in range(2):
                out = jnp.where(diag, near[:, h * half : (h + 1) * half], sent[h])
                grad_w = lax.dynamic_update_slice(grad_w, out, (step * width, h * half))
            for name, (w_part, recv, p) in list(got_w.items()):
                if p // 2 != step:
                    continue
                recv = _tie(recv, prev)
                mine = jnp.where(diag, _tie(w_part, recv), recv)
                ready[name] = (mine, _send(mine, Q_SWAP))
                if name[0] == "y":
                    j = int(name[1:])
                    for which, base in ((0, core * feats), (1, (1 - core) * feats)):
                        w_o = _tie(ready[f"o{j}"][which], prev)
                        w_n = ready[f"y{j}"][which]
                        part = (_dot(grad_blk, w_o) + _dot(g_yc, w_n)).astype(jnp.bfloat16)
                        grad_in = lax.dynamic_update_slice(grad_in, part, (0, base + j * width))
        return grad_in, grad_w

    return jax.shard_map(local_backward, mesh=mesh, in_specs=(io_spec, w_spec, io_spec), out_specs=(io_spec, io_spec), check_vma=False)
```

time: 3490 us -> 1900 us (0.54)
  waiting for transfers between devices: 3140 us -> 523 us
  matrix products: 304 us -> 930 us
  local copies, waits for them, and re-layouts: 0 us -> 238 us
  starting transfers between devices: 0.16 us -> 107 us
  other arithmetic: 32.3 us -> 88.4 us
    reduce_scatter x1 -> x0, waiting for transfers between devices: 1290 us -> none  [local_backward(): lax.psum_scatter(grad_in_part, 'col', scatter_dimension=1, tiled=True)]
    all_gather x2 -> x0, waiting for transfers between devices: 1010 us -> none  [the longest x1 614 us: local_backward(): act_rows = lax.all_gather(act_blk, 'col', axis=1, tiled=True)]
    unnamed x5 -> x0, waiting for transfers between devices: 842 us -> none
    dot_general x2 -> x128, matrix products: 304 us -> 930 us  [the longest x96 655 us: _tdot(): lax.dot_general(a, b, (((0,), (0,)), ((), ())), preferred_element_type=jn...]
    ppermute x0 -> x77, waiting for transfers between devices: none -> 523 us  [_send(): return lax.ppermute(value, AXES, pairs)]
    ppermute x0 -> x77, starting transfers between devices: none -> 107 us  [_send(): return lax.ppermute(value, AXES, pairs)]
    convert_element_type x0 -> x16, local copies, waits for them, and re-layouts: none -> 55.8 us  [local_backward(): part = (_dot(grad_blk, w_o) + _dot(g_yc, w_n)).astype(jnp.bfloat16)]
    unnamed x0 -> x369, local copies, waits for them, and re-layouts: none -> 54.3 us
  transfers between devices with their start and end apart: 4 -> 77, of which waited for: 4 -> 21; matrix products, arithmetic and copies ran while one was open for 10% -> 65% of each run, Pallas kernels for 0% -> 0%
where the time goes in v1:
time: 1900 us; the launch traced here: 1890 us
  matrix products  930 us (49%)
  waiting for transfers between devices  523 us (28%)
  local copies, waits for them, and re-layouts  238 us (13%)
  starting transfers between devices  107 us (6%)
  other arithmetic  88.4 us (5%)
    dot_general x96, matrix products, _tdot(): lax.dot_general(a, b, (((0,), (0,)), ((), ())), preferred_element_type=jn...  655 us
    ppermute x77, waiting for transfers between devices, _send(): return lax.ppermute(value, AXES, pairs)  523 us
    dot_general x32, matrix products, _dot(): lax.dot_general(a, b, (((1,), (0,)), ((), ())), preferred_element_type=jn...  275 us
    ppermute x77, starting transfers between devices, _send(): return lax.ppermute(value, AXES, pairs)  107 us
    convert_element_type x16, local copies, waits for them, and re-layouts, local_backward(): part = (_dot(grad_blk, w_o) + _dot(g_yc, w_n)).astype(jnp.bfloat16)  55.8 us
    unnamed x369, local copies, waits for them, and re-layouts  54.3 us
  transfers between devices with their start and end apart: 77, of which 21 were waited for; matrix products, arithmetic and copies ran while one was open for 65% of the time, Pallas kernels for 0%

profile of v1, /device:TPU:0, one launch (start us, length us, event | category | flops | bytes accessed | tf_op | source)
XLA Modules:
  0.0 1887.7 jit_solution(16837710790012131466)
XLA Ops:
  12.0 23.3 %constant_dynamic-slice_fusion.14 = (bf16[2048,512]{1,0:T(8,128)(2,1)}, bf16[2048,512]{1,0:T(8,128)(2,1)}, bf16[2048,512]{1,0:T(8,128)(2,1)S(1)}, bf16[2048,512]...) fusion(bf16[2048,8192]{1,0:T(8,128)(2,1)} %param.3, ...), kind=kLoop, calls=%fused_computation.155 | loop fusion | bytes 67108928 | tf_op jit(solution)/shard_map/slice | solution.py:63
  39.9 10.7 fusion.44
  50.6 9.7 fusion.53
  164.5 13.7 fusion.31
  377.7 10.5 fusion.45
  388.2 9.8 fusion.54
  417.2 9.6 fusion.72
  426.8 9.7 fusion.83
  454.5 9.6 fusion.96
  464.1 76.3 %collective-permute-done.11 = bf16[2048,1024]{1,0:T(8,128)(2,1)} collective-permute-done((bf16[2048,1024]{1,0:T(8,128)(2,1)}, bf16[2048,1024]{1,0:T(8,128)(2,1)}, u32[]{:S(2)}, u32[]{:S(2)}) %collective-permute-start.11) | collective-permute-done | bytes 4194336 | tf_op jit(solution)/shard_map/ppermute | solution.py:30
  547.7 9.6 fusion.109
  557.3 9.6 fusion.120
  592.2 12.2 add_add_fusion.7
  606.0 26.9 %collective-permute-done.16 = bf16[2048,512]{0,1:T(8,128)(2,1)S(1)} collective-permute-done((bf16[2048,512]{0,1:T(8,128)(2,1)S(1)}, bf16[2048,512]{0,1:T(8,128)(2,1)S(1)}, u32[]{:S(2)}, u32[]{:S(2)}) %collective-permute-start.16) | collective-permute-done | bytes 2097184 | tf_op jit(solution)/shard_map/ppermute | solution.py:30
  661.8 12.2 add_add_fusion.6
  679.7 43.1 %collective-permute-done.23 = bf16[2048,512]{0,1:T(8,128)(2,1)S(1)} collective-permute-done((bf16[2048,512]{0,1:T(8,128)(2,1)S(1)}, bf16[2048,512]{0,1:T(8,128)(2,1)S(1)}, u32[]{:S(2)}, u32[]{:S(2)}) %collective-permute-start.23) | collective-permute-done | bytes 2097184 | tf_op jit(solution)/shard_map/ppermute | solution.py:30
  768.9 12.3 add_add_fusion.5
  781.2 23.9 %collective-permute-done.25 = bf16[2048,512]{0,1:T(8,128)(2,1)} collective-permute-done((bf16[2048,512]{0,1:T(8,128)(2,1)S(1)}, bf16[2048,512]{0,1:T(8,128)(2,1)}, u32[]{:S(2)}, u32[]{:S(2)}) %collective-permute-start.25) | collective-permute-done | bytes 2097184 | tf_op jit(solution)/shard_map/ppermute | solution.py:30
  806.2 44.8 %collective-permute-done.21 = bf16[2048,512]{0,1:T(8,128)(2,1)} collective-permute-done((bf16[2048,512]{0,1:T(8,128)(2,1)}, bf16[2048,512]{0,1:T(8,128)(2,1)}, u32[]{:S(2)}, u32[]{:S(2)}) %collective-permute-start.21) | collective-permute-done | bytes 2097184 | tf_op jit(solution)/shard_map/ppermute | solution.py:30
  884.9 14.1 add_add_fusion.4
  899.1 41.3 %collective-permute-done.30 = bf16[2048,512]{0,1:T(8,128)(2,1)S(1)} collective-permute-done((bf16[2048,512]{0,1:T(8,128)(2,1)}, bf16[2048,512]{0,1:T(8,128)(2,1)S(1)}, u32[]{:S(2)}, u32[]{:S(2)}) %collective-permute-start.30) | collective-permute-done | bytes 2097184 | tf_op jit(solution)/shard_map/ppermute | solution.py:30
  975.3 11.5 dynamic_update_slice.112
  999.8 15.1 collective-permute-done.46
  1019.2 40.6 %collective-permute-done.44 = bf16[2048,512]{0,1:T(8,128)(2,1)S(1)} collective-permute-done((bf16[2048,512]{0,1:T(8,128)(2,1)S(1)}, bf16[2048,512]{0,1:T(8,128)(2,1)S(1)}, u32[]{:S(2)}, u32[]{:S(2)}) %collective-permute-start.44) | collective-permute-done | bytes 2097184 | tf_op jit(solution)/shard_map/ppermute | solution.py:30
  1063.0 9.9 fusion.84
  1111.1 23.0 %collective-permute-done.64 = f32[512,1024]{1,0:T(8,128)S(1)} collective-permute-done((f32[512,1024]{1,0:T(8,128)}, f32[512,1024]{1,0:T(8,128)S(1)}, u32[]{:S(2)}, u32[]{:S(2)}) %collective-permute-start.64) | collective-permute-done | bytes 2097184 | tf_op jit(solution)/shard_map/ppermute | solution.py:30
  1145.2 33.8 %collective-permute-done.65 = f32[512,1024]{1,0:T(8,128)S(1)} collective-permute-done((f32[512,1024]{1,0:T(8,128)}, f32[512,1024]{1,0:T(8,128)S(1)}, u32[]{:S(2)}, u32[]{:S(2)}) %collective-permute-start.65) | collective-permute-done | bytes 2097184 | tf_op jit(solution)/shard_map/ppermute | solution.py:30
  1187.0 11.2 fusion.13
  1198.2 25.0 %collective-permute-done.66 = f32[512,1024]{1,0:T(8,128)} collective-permute-done((f32[512,1024]{1,0:T(8,128)}, f32[512,1024]{1,0:T(8,128)}, u32[]{:S(2)}, u32[]{:S(2)}) %collective-permute-start.66) | collective-permute-done | bytes 2097184 | tf_op jit(solution)/shard_map/ppermute | solution.py:30
  1228.4 11.1 broadcast_in_dim.4
  1245.5 12.2 add_add_fusion.3
  1259.4 14.2 collective-permute-done.36
  1305.9 11.0 add_add_fusion.2
  1318.2 43.9 %collective-permute-done.45 = bf16[2048,512]{0,1:T(8,128)(2,1)S(1)} collective-permute-done((bf16[2048,512]{0,1:T(8,128)(2,1)S(1)}, bf16[2048,512]{0,1:T(8,128)(2,1)S(1)}, u32[]{:S(2)}, u32[]{:S(2)}) %collective-permute-start.45) | collective-permute-done | bytes 2097184 | tf_op jit(solution)/shard_map/ppermute | solution.py:30
  1490.6 11.2 fusion.5
  1507.1 10.1 fusion.7
  1536.4 11.2 fusion.11
  1556.5 11.2 fusion.9
  1567.7 24.2 %collective-permute-done.70 = f32[512,1024]{1,0:T(8,128)} collective-permute-done((f32[512,1024]{1,0:T(8,128)}, f32[512,1024]{1,0:T(8,128)}, u32[]{:S(2)}, u32[]{:S(2)}) %collective-permute-start.70) | collective-permute-done | bytes 2097184 | tf_op jit(solution)/shard_map/ppermute | solution.py:30
  1609.7 14.3 add_add_fusion.1
  1624.0 16.8 collective-permute-done.54
  1701.0 9.9 fusion.6
  1725.8 10.7 fusion.121
  1790.6 11.3 fusion.3
  1808.4 11.2 fusion.1
  1822.6 10.6 add_add_fusion
  1837.8 11.2 fusion
  1849.0 9.9 fusion.2
  (707 shorter events, 1016.1 us)
Async XLA Ops:
  6.7 265.9 %collective-permute-start.6 = (bf16[2048,1024]{1,0:T(8,128)(2,1)}, bf16[2048,1024]{1,0:T(8,128)(2,1)}, u32[]{:S(2)}, u32[]{:S(2)}) collective-permute-start(bf16[2048,1024]{1,0:T(8,128)(2,1)} %get-tuple-element.225), channel_id=1, source_target_pairs={{0,2},{1,3},{4,6},{5,7},{2,0},{3,1},{6,4},{7,5}} | collective-permute-start | bytes 12582920 | tf_op jit(solution)/shard_map/ppermute | solution.py:30
  10.0 168.2 %collective-permute-start.4 = (bf16[2048,1024]{1,0:T(8,128)(2,1)}, bf16[2048,1024]{1,0:T(8,128)(2,1)}, u32[]{:S(2)}, u32[]{:S(2)}) collective-permute-start(bf16[2048,1024]{1,0:T(8,128)(2,1)} %get-tuple-element.225), channel_id=1, source_target_pairs={{0,4},{1,5},{4,0},{5,1},{2,6},{3,7},{6,2},{7,3}} | collective-permute-start | bytes 12582920 | tf_op jit(solution)/shard_map/ppermute | solution.py:30
  11.5 278.2 %collective-permute-start.10 = (bf16[2048,1024]{1,0:T(8,128)(2,1)}, bf16[2048,1024]{1,0:T(8,128)(2,1)}, u32[]{:S(2)}, u32[]{:S(2)}) collective-permute-start(bf16[2048,1024]{1,0:T(8,128)(2,1)} %get-tuple-element.224), channel_id=1, source_target_pairs={{0,2},{1,3},{4,6},{5,7},{2,0},{3,1},{6,4},{7,5}} | collective-permute-start | bytes 12582920 | tf_op jit(solution)/shard_map/ppermute | solution.py:30
  12.0 180.2 %collective-permute-start.1 = (bf16[2048,1024]{1,0:T(8,128)(2,1)}, bf16[2048,1024]{1,0:T(8,128)(2,1)}, u32[]{:S(2)}, u32[]{:S(2)}) collective-permute-start(bf16[2048,1024]{1,0:T(8,128)(2,1)} %get-tuple-element.224), channel_id=1, source_target_pairs={{0,4},{1,5},{4,0},{5,1},{2,6},{3,7},{6,2},{7,3}} | collective-permute-start | bytes 12582920 | tf_op jit(solution)/shard_map/ppermute | solution.py:30
  39.9 260.5 %collective-permute-start.2 = (bf16[2048,512]{0,1:T(8,128)(2,1)}, bf16[2048,512]{0,1:T(8,128)(2,1)}, u32[]{:S(2)}, u32[]{:S(2)}) collective-permute-start(bf16[2048,512]{0,1:T(8,128)(2,1)} %copy.58), channel_id=1, source_target_pairs={{0,1},{1,0},{4,5},{5,4},{2,3},{3,2},{6,7},{7,6}} | collective-permute-start | bytes 6291464 | tf_op jit(solution)/shard_map/ppermute | solution.py:30
  178.2 122.7 %collective-permute-start.5 = (bf16[2048,1024]{1,0:T(8,128)(2,1)}, bf16[2048,1024]{1,0:T(8,128)(2,1)S(1)}, u32[]{:S(2)}, u32[]{:S(2)}) collective-permute-start(bf16[2048,1024]{1,0:T(8,128)(2,1)} %collective-permute-done.4), channel_id=1, source_target_pairs={{0,1},{1,0},{4,5},{5,4},{2,3},{3,2},{6,7},{7,6}} | collective-permute-start | bytes 12582920 | tf_op jit(solution)/shard_map/ppermute | solution.py:30
  192.2 115.7 %collective-permute-start.3 = (bf16[2048,1024]{1,0:T(8,128)(2,1)}, bf16[2048,1024]{1,0:T(8,128)(2,1)}, u32[]{:S(2)}, u32[]{:S(2)}) collective-permute-start(bf16[2048,1024]{1,0:T(8,128)(2,1)} %collective-permute-done.1), channel_id=1, source_target_pairs={{0,1},{1,0},{4,5},{5,4},{2,3},{3,2},{6,7},{7,6}} | collective-permute-start | bytes 12582920 | tf_op jit(solution)/shard_map/ppermute | solution.py:30
  272.5 104.6 %collective-permute-start.17 = (bf16[2048,2048]{1,0:T(8,128)(2,1)S(1)}, bf16[2048,2048]{1,0:T(8,128)(2,1)}, u32[]{:S(2)}, u32[]{:S(2)}) collective-permute-start(bf16[2048,2048]{1,0:T(8,128)(2,1)S(1)} %bitcast.326), channel_id=1, source_target_pairs={{0,1},{1,0},{4,5},{5,4},{2,3},{3,2},{6,7},{7,6}} | collective-permute-start | bytes 25165832 | tf_op jit(solution)/shard_map/ppermute | solution.py:30
  315.2 121.3 %collective-permute-start = (bf16[2048,512]{0,1:T(8,128)(2,1)S(1)}, bf16[2048,512]{0,1:T(8,128)(2,1)S(1)}, u32[]{:S(2)}, u32[]{:S(2)}) collective-permute-start(bf16[2048,512]{0,1:T(8,128)(2,1)S(1)} %copy-done.75), channel_id=1, source_target_pairs={{0,2},{1,3},{4,6},{5,7},{2,0},{3,1},{6,4},{7,5}} | collective-permute-start | bytes 6291464 | tf_op jit(solution)/shard_map/ppermute | solution.py:30
  355.3 95.5 %collective-permute-start.7 = (bf16[2048,1024]{1,0:T(8,128)(2,1)}, bf16[2048,1024]{1,0:T(8,128)(2,1)S(1)}, u32[]{:S(2)}, u32[]{:S(2)}) collective-permute-start(bf16[2048,1024]{1,0:T(8,128)(2,1)} %collective-permute-done.6), channel_id=1, source_target_pairs={{4,0},{5,1},{2,6},{3,7}} | collective-permute-start | bytes 12582920 | tf_op jit(solution)/shard_map/ppermute | solution.py:30
  366.3 174.1 %collective-permute-start.11 = (bf16[2048,1024]{1,0:T(8,128)(2,1)}, bf16[2048,1024]{1,0:T(8,128)(2,1)}, u32[]{:S(2)}, u32[]{:S(2)}) collective-permute-start(bf16[2048,1024]{1,0:T(8,128)(2,1)} %collective-permute-done.10), channel_id=1, source_target_pairs={{4,0},{5,1},{2,6},{3,7}} | collective-permute-start | bytes 12582920 | tf_op jit(solution)/shard_map/ppermute | solution.py:30
  377.2 163.7 %collective-permute-start.18 = (bf16[2048,1024]{1,0:T(8,128)(2,1)}, bf16[2048,1024]{1,0:T(8,128)(2,1)S(1)}, u32[]{:S(2)}, u32[]{:S(2)}) collective-permute-start(bf16[2048,1024]{1,0:T(8,128)(2,1)} %collective-permute-done.6), channel_id=1, source_target_pairs={{0,1},{1,0},{4,5},{5,4},{2,3},{3,2},{6,7},{7,6}} | collective-permute-start | bytes 12582920 | tf_op jit(solution)/shard_map/ppermute | solution.py:30
  398.0 145.5 %collective-permute-start.19 = (bf16[2048,1024]{1,0:T(8,128)(2,1)}, bf16[2048,1024]{1,0:T(8,128)(2,1)S(1)}, u32[]{:S(2)}, u32[]{:S(2)}) collective-permute-start(bf16[2048,1024]{1,0:T(8,128)(2,1)} %collective-permute-done.10), channel_id=1, source_target_pairs={{0,1},{1,0},{4,5},{5,4},{2,3},{3,2},{6,7},{7,6}} | collective-permute-start | bytes 12582920 | tf_op jit(solution)/shard_map/ppermute | solution.py:30
  436.5 130.4 %collective-permute-start.8 = (bf16[2048,512]{0,1:T(8,128)(2,1)S(1)}, bf16[2048,512]{0,1:T(8,128)(2,1)S(1)}, u32[]{:S(2)}, u32[]{:S(2)}) collective-permute-start(bf16[2048,512]{0,1:T(8,128)(2,1)S(1)} %copy-done.71), channel_id=1, source_target_pairs={{0,2},{1,3},{4,7},{5,6},{2,1},{3,0},{6,4},{7,5}} | collective-permute-start | bytes 6291464 | tf_op jit(solution)/shard_map/ppermute | solution.py:30
  450.9 116.4 %collective-permute-start.9 = (bf16[2048,1024]{1,0:T(8,128)(2,1)S(1)}, bf16[2048,1024]{1,0:T(8,128)(2,1)}, u32[]{:S(2)}, u32[]{:S(2)}) collective-permute-start(bf16[2048,1024]{1,0:T(8,128)(2,1)S(1)} %collective-permute-done.7), channel_id=1, source_target_pairs={{0,1},{1,0},{4,5},{5,4},{2,3},{3,2},{6,7},{7,6}} | collective-permute-start | bytes 12582920 | tf_op jit(solution)/shard_map/ppermute | solution.py:30
  543.5 89.4 %collective-permute-start.16 = (bf16[2048,512]{0,1:T(8,128)(2,1)S(1)}, bf16[2048,512]{0,1:T(8,128)(2,1)S(1)}, u32[]{:S(2)}, u32[]{:S(2)}) collective-permute-start(bf16[2048,512]{0,1:T(8,128)(2,1)S(1)} %copy-done.67), channel_id=1, source_target_pairs={{0,2},{1,3},{4,6},{5,7},{2,0},{3,1},{6,4},{7,5}} | collective-permute-start | bytes 6291464 | tf_op jit(solution)/shard_map/ppermute | solution.py:30
  566.8 111.4 %collective-permute-start.24 = (bf16[2048,512]{0,1:T(8,128)(2,1)S(1)}, bf16[2048,512]{0,1:T(8,128)(2,1)S(1)}, u32[]{:S(2)}, u32[]{:S(2)}) collective-permute-start(bf16[2048,512]{0,1:T(8,128)(2,1)S(1)} %copy-done.66), channel_id=1, source_target_pairs={{0,2},{1,3},{4,7},{5,6},{2,1},{3,0},{6,4},{7,5}} | collective-permute-start | bytes 6291464 | tf_op jit(solution)/shard_map/ppermute | solution.py:30
  567.3 155.5 %collective-permute-start.23 = (bf16[2048,512]{0,1:T(8,128)(2,1)S(1)}, bf16[2048,512]{0,1:T(8,128)(2,1)S(1)}, u32[]{:S(2)}, u32[]{:S(2)}) collective-permute-start(bf16[2048,512]{0,1:T(8,128)(2,1)S(1)} %copy-done.65), channel_id=1, source_target_pairs={{0,2},{1,3},{4,6},{5,7},{2,0},{3,1},{6,4},{7,5}} | collective-permute-start | bytes 6291464 | tf_op jit(solution)/shard_map/ppermute | solution.py:30
  579.0 177.0 %collective-permute-start.14 = (bf16[2048,512]{0,1:T(8,128)(2,1)S(1)}, bf16[2048,512]{0,1:T(8,128)(2,1)S(1)}, u32[]{:S(2)}, u32[]{:S(2)}) collective-permute-start(bf16[2048,512]{0,1:T(8,128)(2,1)S(1)} %copy-done.6), channel_id=1, source_target_pairs={{4,0},{5,1},{2,6},{3,7}} | collective-permute-start | bytes 6291464 | tf_op jit(solution)/shard_map/ppermute | solution.py:30
  604.4 161.6 %collective-permute-start.29 = (bf16[2048,512]{0,1:T(8,128)(2,1)S(1)}, bf16[2048,512]{0,1:T(8,128)(2,1)S(1)}, u32[]{:S(2)}, u32[]{:S(2)}) collective-permute-start(bf16[2048,512]{0,1:T(8,128)(2,1)S(1)} %copy-done.5), channel_id=1, source_target_pairs={{4,0},{5,1},{2,6},{3,7}} | collective-permute-start | bytes 6291464 | tf_op jit(solution)/shard_map/ppermute | solution.py:30
  632.9 353.9 %collective-permute-start.37 = (bf16[2048,512]{0,1:T(8,128)(2,1)}, bf16[2048,512]{0,1:T(8,128)(2,1)}, u32[]{:S(2)}, u32[]{:S(2)}) collective-permute-start(bf16[2048,512]{0,1:T(8,128)(2,1)} %get-tuple-element.146), channel_id=1, source_target_pairs={{4,0},{5,1},{2,6},{3,7}} | collective-permute-start | bytes 6291464 | tf_op jit(solution)/shard_map/ppermute | solution.py:30
  678.2 313.3 %collective-permute-start.35 = (bf16[2048,512]{0,1:T(8,128)(2,1)S(1)}, bf16[2048,512]{0,1:T(8,128)(2,1)S(1)}, u32[]{:S(2)}, u32[]{:S(2)}) collective-permute-start(bf16[2048,512]{0,1:T(8,128)(2,1)S(1)} %copy-done.2), channel_id=1, source_target_pairs={{4,0},{5,1},{2,6},{3,7}} | collective-permute-start | bytes 6291464 | tf_op jit(solution)/shard_map/ppermute | solution.py:30
  752.5 219.6 %collective-permute-start.61 = (f32[512,1024]{1,0:T(8,128)}, f32[512,1024]{1,0:T(8,128)S(1)}, u32[]{:S(2)}, u32[]{:S(2)}) collective-permute-start(f32[512,1024]{1,0:T(8,128)} %add_add_fusion.23), channel_id=1, source_target_pairs={{0,4},{1,5},{6,2},{7,3}} | collective-permute-start | bytes 6291464 | tf_op jit(solution)/shard_map/ppermute | solution.py:30
  766.0 85.0 %collective-permute-start.21 = (bf16[2048,512]{0,1:T(8,128)(2,1)}, bf16[2048,512]{0,1:T(8,128)(2,1)}, u32[]{:S(2)}, u32[]{:S(2)}) collective-permute-start(bf16[2048,512]{0,1:T(8,128)(2,1)} %broadcast_select_fusion.26), channel_id=1, source_target_pairs={{0,2},{1,3},{4,6},{5,7},{2,0},{3,1},{6,4},{7,5}} | collective-permute-start | bytes 6291464 | tf_op jit(solution)/shard_map/ppermute | solution.py:30
  805.1 93.9 %collective-permute-start.31 = (bf16[2048,512]{0,1:T(8,128)(2,1)S(1)}, bf16[2048,512]{0,1:T(8,128)(2,1)S(1)}, u32[]{:S(2)}, u32[]{:S(2)}) collective-permute-start(bf16[2048,512]{0,1:T(8,128)(2,1)S(1)} %copy-done.60), channel_id=1, source_target_pairs={{0,2},{1,3},{4,7},{5,6},{2,1},{3,0},{6,4},{7,5}} | collective-permute-start | bytes 6291464 | tf_op jit(solution)/shard_map/ppermute | solution.py:30
  851.0 89.3 %collective-permute-start.30 = (bf16[2048,512]{0,1:T(8,128)(2,1)}, bf16[2048,512]{0,1:T(8,128)(2,1)S(1)}, u32[]{:S(2)}, u32[]{:S(2)}) collective-permute-start(bf16[2048,512]{0,1:T(8,128)(2,1)} %broadcast_select_fusion.20), channel_id=1, source_target_pairs={{0,2},{1,3},{4,6},{5,7},{2,0},{3,1},{6,4},{7,5}} | collective-permute-start | bytes 6291464 | tf_op jit(solution)/shard_map/ppermute | solution.py:30
  965.8 94.0 %collective-permute-start.44 = (bf16[2048,512]{0,1:T(8,128)(2,1)S(1)}, bf16[2048,512]{0,1:T(8,128)(2,1)S(1)}, u32[]{:S(2)}, u32[]{:S(2)}) collective-permute-start(bf16[2048,512]{0,1:T(8,128)(2,1)S(1)} %copy-done), channel_id=1, source_target_pairs={{4,0},{5,1},{2,6},{3,7}} | collective-permute-start | bytes 6291464 | tf_op jit(solution)/shard_map/ppermute | solution.py:30
  972.2 486.9 %collective-permute-start.55 = (bf16[2048,512]{0,1:T(8,128)(2,1)}, bf16[2048,512]{0,1:T(8,128)(2,1)}, u32[]{:S(2)}, u32[]{:S(2)}) collective-permute-start(bf16[2048,512]{0,1:T(8,128)(2,1)} %get-tuple-element.186), channel_id=1, source_target_pairs={{4,0},{5,1},{2,6},{3,7}} | collective-permute-start | bytes 6291464 | tf_op jit(solution)/shard_map/ppermute | solution.py:30
  986.8 482.8 %collective-permute-start.53 = (bf16[2048,512]{0,1:T(8,128)(2,1)}, bf16[2048,512]{0,1:T(8,128)(2,1)}, u32[]{:S(2)}, u32[]{:S(2)}) collective-permute-start(bf16[2048,512]{0,1:T(8,128)(2,1)} %get-tuple-element.173), channel_id=1, source_target_pairs={{4,0},{5,1},{2,6},{3,7}} | collective-permute-start | bytes 6291464 | tf_op jit(solution)/shard_map/ppermute | solution.py:30
  991.6 81.4 %collective-permute-start.62 = (f32[512,1024]{1,0:T(8,128)S(1)}, f32[512,1024]{1,0:T(8,128)S(1)}, u32[]{:S(2)}, u32[]{:S(2)}) collective-permute-start(f32[512,1024]{1,0:T(8,128)S(1)} %copy-done.93), channel_id=1, source_target_pairs={{0,4},{1,5},{6,2},{7,3}} | collective-permute-start | bytes 6291464 | tf_op jit(solution)/shard_map/ppermute | solution.py:30
  1072.9 106.1 %collective-permute-start.65 = (f32[512,1024]{1,0:T(8,128)}, f32[512,1024]{1,0:T(8,128)S(1)}, u32[]{:S(2)}, u32[]{:S(2)}) collective-permute-start(f32[512,1024]{1,0:T(8,128)} %add_add_fusion.19), channel_id=1, source_target_pairs={{0,4},{1,5},{6,2},{7,3}} | collective-permute-start | bytes 6291464 | tf_op jit(solution)/shard_map/ppermute | solution.py:30
  1090.3 132.9 %collective-permute-start.66 = (f32[512,1024]{1,0:T(8,128)}, f32[512,1024]{1,0:T(8,128)}, u32[]{:S(2)}, u32[]{:S(2)}) collective-permute-start(f32[512,1024]{1,0:T(8,128)} %add_add_fusion.18), channel_id=1, source_target_pairs={{0,4},{1,5},{6,2},{7,3}} | collective-permute-start | bytes 6291464 | tf_op jit(solution)/shard_map/ppermute | solution.py:30
  1134.1 255.8 %collective-permute-start.50 = (bf16[2048,512]{0,1:T(8,128)(2,1)}, bf16[2048,512]{0,1:T(8,128)(2,1)}, u32[]{:S(2)}, u32[]{:S(2)}) collective-permute-start(bf16[2048,512]{0,1:T(8,128)(2,1)} %broadcast_select_fusion.7), channel_id=1, source_target_pairs={{0,1},{1,0},{4,5},{5,4},{2,3},{3,2},{6,7},{7,6}} | collective-permute-start | bytes 6291464 | tf_op jit(solution)/shard_map/ppermute | solution.py:30
  1179.1 78.7 %collective-permute-start.38 = (bf16[2048,512]{0,1:T(8,128)(2,1)}, bf16[2048,512]{0,1:T(8,128)(2,1)}, u32[]{:S(2)}, u32[]{:S(2)}) collective-permute-start(bf16[2048,512]{0,1:T(8,128)(2,1)} %broadcast_select_fusion.15), channel_id=1, source_target_pairs={{0,2},{1,3},{4,7},{5,6},{2,1},{3,0},{6,4},{7,5}} | collective-permute-start | bytes 6291464 | tf_op jit(solution)/shard_map/ppermute | solution.py:30
  1273.5 88.5 %collective-permute-start.45 = (bf16[2048,512]{0,1:T(8,128)(2,1)S(1)}, bf16[2048,512]{0,1:T(8,128)(2,1)S(1)}, u32[]{:S(2)}, u32[]{:S(2)}) collective-permute-start(bf16[2048,512]{0,1:T(8,128)(2,1)S(1)} %copy-done.79), channel_id=1, source_target_pairs={{0,2},{1,3},{4,6},{5,7},{2,0},{3,1},{6,4},{7,5}} | collective-permute-start | bytes 6291464 | tf_op jit(solution)/shard_map/ppermute | solution.py:30
  1317.9 90.5 %collective-permute-start.48 = (bf16[2048,512]{0,1:T(8,128)(2,1)S(1)}, bf16[2048,512]{0,1:T(8,128)(2,1)}, u32[]{:S(2)}, u32[]{:S(2)}) collective-permute-start(bf16[2048,512]{0,1:T(8,128)(2,1)S(1)} %copy-done.64), channel_id=1, source_target_pairs={{0,1},{1,0},{4,5},{5,4},{2,3},{3,2},{6,7},{7,6}} | collective-permute-start | bytes 6291464 | tf_op jit(solution)/shard_map/ppermute | solution.py:30
  1408.4 76.9 %collective-permute-start.67 = (f32[512,1024]{1,0:T(8,128)S(1)}, f32[512,1024]{1,0:T(8,128)S(1)}, u32[]{:S(2)}, u32[]{:S(2)}) collective-permute-start(f32[512,1024]{1,0:T(8,128)S(1)} %copy-done.92), channel_id=1, source_target_pairs={{0,4},{1,5},{6,2},{7,3}} | collective-permute-start | bytes 6291464 | tf_op jit(solution)/shard_map/ppermute | solution.py:30
  1443.6 104.1 %collective-permute-start.69 = (f32[512,1024]{1,0:T(8,128)}, f32[512,1024]{1,0:T(8,128)}, u32[]{:S(2)}, u32[]{:S(2)}) collective-permute-start(f32[512,1024]{1,0:T(8,128)} %add_add_fusion.15), channel_id=1, source_target_pairs={{0,4},{1,5},{6,2},{7,3}} | collective-permute-start | bytes 6291464 | tf_op jit(solution)/shard_map/ppermute | solution.py:30
  1469.7 122.3 %collective-permute-start.70 = (f32[512,1024]{1,0:T(8,128)}, f32[512,1024]{1,0:T(8,128)}, u32[]{:S(2)}, u32[]{:S(2)}) collective-permute-start(f32[512,1024]{1,0:T(8,128)} %add_add_fusion.14), channel_id=1, source_target_pairs={{0,4},{1,5},{6,2},{7,3}} | collective-permute-start | bytes 6291464 | tf_op jit(solution)/shard_map/ppermute | solution.py:30
  1485.3 227.0 %collective-permute-start.59 = (bf16[2048,512]{0,1:T(8,128)(2,1)}, bf16[2048,512]{0,1:T(8,128)(2,1)}, u32[]{:S(2)}, u32[]{:S(2)}) collective-permute-start(bf16[2048,512]{0,1:T(8,128)(2,1)} %broadcast_select_fusion.1), channel_id=1, source_target_pairs={{0,1},{1,0},{4,5},{5,4},{2,3},{3,2},{6,7},{7,6}} | collective-permute-start | bytes 6291464 | tf_op jit(solution)/shard_map/ppermute | solution.py:30
  1502.1 212.9 %collective-permute-start.57 = (bf16[2048,512]{0,1:T(8,128)(2,1)}, bf16[2048,512]{0,1:T(8,128)(2,1)}, u32[]{:S(2)}, u32[]{:S(2)}) collective-permute-start(bf16[2048,512]{0,1:T(8,128)(2,1)} %broadcast_select_fusion.5), channel_id=1, source_target_pairs={{0,1},{1,0},{4,5},{5,4},{2,3},{3,2},{6,7},{7,6}} | collective-permute-start | bytes 6291464 | tf_op jit(solution)/shard_map/ppermute | solution.py:30
  1517.1 219.3 %collective-permute-start.71 = (f32[512,1024]{1,0:T(8,128)}, f32[512,1024]{1,0:T(8,128)}, u32[]{:S(2)}, u32[]{:S(2)}) collective-permute-start(f32[512,1024]{1,0:T(8,128)} %add_add_fusion.13), channel_id=1, source_target_pairs={{0,4},{1,5},{6,2},{7,3}} | collective-permute-start | bytes 6291464 | tf_op jit(solution)/shard_map/ppermute | solution.py:30
  1547.7 76.3 %collective-permute-start.56 = (bf16[2048,512]{0,1:T(8,128)(2,1)}, bf16[2048,512]{0,1:T(8,128)(2,1)}, u32[]{:S(2)}, u32[]{:S(2)}) collective-permute-start(bf16[2048,512]{0,1:T(8,128)(2,1)} %broadcast_select_fusion.3), channel_id=1, source_target_pairs={{0,2},{1,3},{4,7},{5,6},{2,1},{3,0},{6,4},{7,5}} | collective-permute-start | bytes 6291464 | tf_op jit(solution)/shard_map/ppermute | solution.py:30
  1656.8 99.9 %collective-permute-start.72 = (f32[512,1024]{1,0:T(8,128)}, f32[512,1024]{1,0:T(8,128)}, u32[]{:S(2)}, u32[]{:S(2)}) collective-permute-start(f32[512,1024]{1,0:T(8,128)} %add_add_fusion.12), channel_id=1, source_target_pairs={{0,4},{1,5},{6,2},{7,3}} | collective-permute-start | bytes 6291464 | tf_op jit(solution)/shard_map/ppermute | solution.py:30
  1698.2 103.7 %collective-permute-start.73 = (f32[512,1024]{1,0:T(8,128)}, f32[512,1024]{1,0:T(8,128)}, u32[]{:S(2)}, u32[]{:S(2)}) collective-permute-start(f32[512,1024]{1,0:T(8,128)} %add_add_fusion.11), channel_id=1, source_target_pairs={{0,4},{1,5},{6,2},{7,3}} | collective-permute-start | bytes 6291464 | tf_op jit(solution)/shard_map/ppermute | solution.py:30
  1712.3 107.3 %collective-permute-start.74 = (f32[512,1024]{1,0:T(8,128)}, f32[512,1024]{1,0:T(8,128)}, u32[]{:S(2)}, u32[]{:S(2)}) collective-permute-start(f32[512,1024]{1,0:T(8,128)} %add_add_fusion.10), channel_id=1, source_target_pairs={{0,4},{1,5},{6,2},{7,3}} | collective-permute-start | bytes 6291464 | tf_op jit(solution)/shard_map/ppermute | solution.py:30
  1736.5 137.1 %collective-permute-start.75 = (f32[512,1024]{1,0:T(8,128)}, f32[512,1024]{1,0:T(8,128)}, u32[]{:S(2)}, u32[]{:S(2)}) collective-permute-start(f32[512,1024]{1,0:T(8,128)} %add_add_fusion.9), channel_id=1, source_target_pairs={{0,4},{1,5},{6,2},{7,3}} | collective-permute-start | bytes 6291464 | tf_op jit(solution)/shard_map/ppermute | solution.py:30
  1756.8 129.0 %collective-permute-start.76 = (f32[512,1024]{1,0:T(8,128)}, f32[512,1024]{1,0:T(8,128)}, u32[]{:S(2)}, u32[]{:S(2)}) collective-permute-start(f32[512,1024]{1,0:T(8,128)} %add_add_fusion.8), channel_id=1, source_target_pairs={{0,4},{1,5},{6,2},{7,3}} | collective-permute-start | bytes 6291464 | tf_op jit(solution)/shard_map/ppermute | solution.py:30
  (208 other events, 4417.5 us)

commit v2 on v0

v2 whole, which is shorter than its diff:
```python
import jax
import jax.numpy as jnp
from jax import lax
from jax.sharding import PartitionSpec as P


CHUNKS = 8
AHEAD = 5
AXES = ("col", "row")
W_ORDER = ("o0", "o1", "o2", "o3", "o4", "y0", "o5", "y1", "o6", "y2", "o7", "y3", "y4", "y5", "y6", "y7")


def _dev(x, y, q):
    return y * 4 + x * 2 + q


def _chips():
    return [(x, y, q) for x in (0, 1) for y in (0, 1) for q in (0, 1)]


Y_SWAP = [(_dev(x, y, q), _dev(x, 1 - y, q)) for x, y, q in _chips()]
X_SWAP = [(_dev(x, y, q), _dev(1 - x, y, q)) for x, y, q in _chips()]
X_CROSS = [(_dev(x, y, q), _dev(1 - x, y, q if x == y else 1 - q)) for x, y, q in _chips()]
Q_SWAP = [(_dev(x, y, q), _dev(x, y, 1 - q)) for x, y, q in _chips()]
Y_TO_DIAG = [pair for pair, (x, y, q) in zip(Y_SWAP, _chips()) if x != y]
Y_FROM_DIAG = [pair for pair, (x, y, q) in zip(Y_SWAP, _chips()) if x == y]


def _send(value, pairs):
    return lax.ppermute(value, AXES, pairs)


def _tie(value, *deps):
    deps = tuple(d for d in deps if d is not None)
    if not deps:
        return value
    return lax.optimization_barrier((value,) + deps)[0]


def _mm(a, b, over=0):
    return lax.dot_general(a, b, (((1,), (over,)), ((), ())), preferred_element_type=jnp.float32)


def solution(mesh):
    io_spec = P(("dp", "row"), "col")
    w_spec = P("row", "col")

    def local_backward(act_blk, w_blk, grad_blk):
        row = lax.axis_index("row")
        col = lax.axis_index("col")
        core = row % 2
        diag = (row // 2) == col
        tokens, wide = act_blk.shape
        feats, outs = w_blk.shape
        width = feats // CHUNKS

        def cut(a, j):
            return a[j * width : (j + 1) * width]

        g_x = _send(grad_blk, X_SWAP)
        g_y = _send(grad_blk, Y_SWAP)
        g_q = _send(grad_blk, Q_SWAP)

        x_same = lax.dynamic_slice(act_blk, (0, core * feats), (tokens, feats)).T
        x_other = lax.dynamic_slice(act_blk, (0, (1 - core) * feats), (tokens, feats)).T
        x_q = _send(x_other, Q_SWAP)
        near_own = _mm(x_same, grad_blk) + _mm(x_q, g_q)
        g_x, g_y = _tie(g_x, near_own), _tie(g_y, near_own)
        g_d = _send(g_x, Y_TO_DIAG)

        w_y = [_send(_tie(cut(w_blk, j), g_x), Y_TO_DIAG) for j in range(CHUNKS)]
        got, got_w = [], {}

        def exchange(p, dep=None):
            name = W_ORDER[p]
            j = int(name[1:])
            w_part = cut(w_blk, j) if name[0] == "o" else w_y[j]
            x_part = cut(x_same if p % 2 == 0 else x_other, p // 2)
            if name[0] == "o":
                load = _tie(jnp.where(diag, w_part, x_part), dep)
            else:
                load = jnp.where(diag, w_part, _tie(x_part, dep))
            got.append(_send(load, X_SWAP if p % 2 == 0 else X_CROSS))
            got_w[name] = (w_part, got[-1], p)

        for p in range(AHEAD):
            exchange(p)

        g_yq = _send(g_y, Q_SWAP)
        g_xx = jnp.concatenate([g_x, _send(g_x, Q_SWAP)], axis=0)
        far_own = _mm(x_same, g_y) + _mm(x_q, g_yq)
        g_all = jnp.concatenate([grad_blk, g_y], axis=1)
        g_d = _tie(g_d, far_own, g_xx, g_all)
        g_dd = jnp.concatenate([g_d, _send(g_d, Q_SWAP)], axis=0)

        def put(out, j, both):
            for w_full, base in zip(both, (core * feats, (1 - core) * feats)):
                part = _mm(g_all, w_full, over=1).astype(jnp.bfloat16)
                out = lax.dynamic_update_slice(out, part, (0, base + j * width))
            return out

        grad_in = jnp.zeros((tokens, wide), jnp.bfloat16)
        grad_w = jnp.zeros((feats, outs), jnp.float32)
        last, pending, landed = far_own, [], []

        def store(out, step, near, sent):
            return lax.dynamic_update_slice(out, jnp.where(diag, near, sent), (step * width, 0))

        for step in range(CHUNKS):
            grad_in, r1, r2, _ = lax.optimization_barrier((grad_in, got[2 * step], got[2 * step + 1], last))
            x_far = jnp.concatenate([r1, r2], axis=1)
            far = cut(far_own, step) + _mm(x_far, g_dd)
            sent = _send(far, Y_FROM_DIAG)
            while len(got) < min(2 * step + AHEAD + 1, 2 * CHUNKS):
                exchange(len(got), far)
            near = cut(near_own, step) + _mm(_tie(x_far, far), g_xx)
            last = near
            landed.append((step, near, sent))
            if step < CHUNKS - 3:
                grad_w = store(grad_w, *landed.pop(0))
            for j, both in pending:
                grad_in = put(grad_in, j, both)
            pending = []
            for name, (w_n, recv_n, p) in list(got_w.items()):
                if p // 2 != step or name[0] != "y":
                    continue
                j = int(name[1:])
                w_o, recv_o, _ = got_w[f"o{j}"]
                recv_o, recv_n = _tie(recv_o, far), _tie(recv_n, far)
                mine = jnp.concatenate(
                    [jnp.where(diag, _tie(w_o, recv_o), recv_o), jnp.where(diag, _tie(w_n, recv_n), recv_n)], axis=1
                )
                pending.append((j, (mine, _send(mine, Q_SWAP))))
        for j, both in pending:
            grad_in = put(grad_in, j, both)
        for step, near, sent in landed:
            grad_in, sent = lax.optimization_barrier((grad_in, sent))
            grad_w = store(grad_w, step, near, sent)
        return grad_in, grad_w

    return jax.shard_map(local_backward, mesh=mesh, in_specs=(io_spec, w_spec, io_spec), out_specs=(io_spec, io_spec), check_vma=False)
```

time: 3490 us -> 1760 us (0.50)
  waiting for transfers between devices: 3140 us -> 741 us
  matrix products: 304 us -> 644 us
  local copies, waits for them, and re-layouts: 0 us -> 165 us
  other arithmetic: 32.3 us -> 116 us
  starting transfers between devices: 0.16 us -> 78 us
    reduce_scatter x1 -> x0, waiting for transfers between devices: 1290 us -> none  [local_backward(): lax.psum_scatter(grad_in_part, 'col', scatter_dimension=1, tiled=True)]
    all_gather x2 -> x0, waiting for transfers between devices: 1010 us -> none  [the longest x1 614 us: local_backward(): act_rows = lax.all_gather(act_blk, 'col', axis=1, tiled=True)]
    unnamed x5 -> x0, waiting for transfers between devices: 842 us -> none
    ppermute x0 -> x48, waiting for transfers between devices: none -> 741 us  [_send(): return lax.ppermute(value, AXES, pairs)]
    dot_general x2 -> x36, matrix products: 304 us -> 644 us  [_mm(): lax.dot_general(a, b, (((1,), (over,)), ((), ())), preferred_element_type...]
    unnamed x0 -> x95, local copies, waits for them, and re-layouts: none -> 87.4 us
    ppermute x0 -> x48, starting transfers between devices: none -> 78 us  [_send(): return lax.ppermute(value, AXES, pairs)]
    select_n x0 -> x21, other arithmetic: none -> 38.7 us  [the longest x8 19.4 us: exchange(): load = jnp.where(diag, w_part, _tie(x_part, dep))]
  transfers between devices with their start and end apart: 4 -> 48, of which waited for: 4 -> 20; matrix products, arithmetic and copies ran while one was open for 10% -> 49% of each run, Pallas kernels for 0% -> 0%
where the time goes in v2:
time: 1760 us; the launch traced here: 1750 us
  waiting for transfers between devices  741 us (42%)
  matrix products  644 us (37%)
  local copies, waits for them, and re-layouts  165 us (9%)
  other arithmetic  116 us (7%)
  starting transfers between devices  78 us (4%)
    ppermute x48, waiting for transfers between devices, _send(): return lax.ppermute(value, AXES, pairs)  741 us
    dot_general x36, matrix products, _mm(): lax.dot_general(a, b, (((1,), (over,)), ((), ())), preferred_element_type...  644 us
    unnamed x95, local copies, waits for them, and re-layouts  87.4 us
    ppermute x48, starting transfers between devices, _send(): return lax.ppermute(value, AXES, pairs)  78 us
    slice x2, other arithmetic, cut(): return a[j * width:(j + 1) * width]  37.6 us
  transfers between devices with their start and end apart: 48, of which 20 were waited for; matrix products, arithmetic and copies ran while one was open for 49% of the time, Pallas kernels for 0%

profile of v2, /device:TPU:0, one launch (start us, length us, event | category | flops | bytes accessed | tf_op | source)
XLA Modules:
  0.0 1746.5 jit_solution(321110981322409646)
XLA Ops:
  0.7 23.3 %constant_dynamic-slice_fusion = (bf16[2048,4096]{1,0:T(8,128)(2,1)}, bf16[2048,4096]{1,0:T(8,128)(2,1)}) fusion(bf16[2048,8192]{1,0:T(8,128)(2,1)} %param.3, s32[]{:T(128)S(6)} %select_n.232, s32[]{:T(128)S(6)} %select_n.230), kind=kLoop, calls=%fused_computation.121 | loop fusion | bytes 67108872 | tf_op jit(solution)/shard_map/dynamic_slice | solution.py:65
  23.9 22.5 %copy.8 = bf16[2048,4096]{0,1:T(8,128)(2,1)} copy(bf16[2048,4096]{1,0:T(8,128)(2,1)} %get-tuple-element.194) | data formatting | bytes 33554432
  51.8 43.9 %fusion.20 = f32[4096,2048]{1,0:T(8,128)} fusion(bf16[2048,4096]{1,0:T(8,128)(2,1)} %get-tuple-element.195, bf16[2048,2048]{1,0:T(8,128)(2,1)} %param.5), kind=kOutput, calls=%fused_computation.125 | convolution fusion | flops 34359738368 | bytes 58720256 | tf_op jit(solution)/shard_map/dot_general | solution.py:41
  95.7 50.6 %convolution_add_fusion = f32[4096,2048]{1,0:T(8,128)} fusion(f32[4096,2048]{1,0:T(8,128)} %fusion.20, bf16[4096,2048]{1,0:T(8,128)(2,1)S(1)} %collective-permute-done.3, bf16[2048,2048]{1,0:T(8,128)(2,1)} %collective-permute-done.4), kind=kOutput, calls=%fused_computation | convolution fusion | flops 34368126976 | bytes 92274688 | tf_op jit(solution)/shard_map/dot_general | solution.py:41
  146.3 84.9 %collective-permute-done.2 = bf16[2048,2048]{1,0:T(8,128)(2,1)} collective-permute-done((bf16[2048,2048]{1,0:T(8,128)(2,1)}, bf16[2048,2048]{1,0:T(8,128)(2,1)}, u32[]{:S(2)}, u32[]{:S(2)}) %collective-permute-start.2) | collective-permute-done | bytes 8388640 | tf_op jit(solution)/shard_map/ppermute | solution.py:30
  258.9 43.5 %fusion.21 = f32[4096,2048]{1,0:T(8,128)} fusion(bf16[4096,2048]{1,0:T(8,128)(2,1)} %copy-done.40, bf16[2048,2048]{1,0:T(8,128)(2,1)} %collective-permute-done.5), kind=kOutput, calls=%fused_computation.126 | convolution fusion | flops 34359738368 | bytes 58720256 | tf_op jit(solution)/shard_map/dot_general | solution.py:41
  310.7 46.4 %convolution_add_fusion.1 = f32[4096,2048]{1,0:T(8,128)} fusion(f32[4096,2048]{1,0:T(8,128)} %fusion.21, bf16[2048,4096]{1,0:T(8,128)(2,1)} %get-tuple-element.195, bf16[2048,2048]{1,0:T(8,128)(2,1)} %collective-permute-done.2), kind=kOutput, calls=%fused_computation.1 | convolution fusion | flops 34368126976 | bytes 92274688 | tf_op jit(solution)/shard_map/dot_general | solution.py:41
  357.1 68.8 %collective-permute-done.9 = bf16[2048,2048]{1,0:T(8,128)(2,1)} collective-permute-done((bf16[2048,2048]{1,0:T(8,128)(2,1)}, bf16[2048,2048]{1,0:T(8,128)(2,1)}, u32[]{:S(2)}, u32[]{:S(2)}) %collective-permute-start.9) | collective-permute-done | bytes 8388640 | tf_op jit(solution)/shard_map/ppermute | solution.py:30
  426.0 22.4 %copy.7 = bf16[2048,4096]{0,1:T(8,128)(2,1)} copy(bf16[2048,4096]{1,0:T(8,128)(2,1)} %get-tuple-element.195) | data formatting | bytes 33554432
  448.4 15.6 fusion.19
  464.1 22.0 %fusion.18 = (bf16[512,2048]{1,0:T(8,128)(2,1)}, bf16[512,2048]{1,0:T(8,128)(2,1)}, bf16[512,2048]{1,0:T(8,128)(2,1)}, bf16[512,2048]{1,0:T(8,128)(2,1)}, bf16[5...) fusion(bf16[4096,2048]{1,0:T(8,128)(2,1)} %bitcast.67, ...), kind=kLoop, calls=%fused_computation.123 | loop fusion | flops 2097152 | bytes 67108864 | tf_op jit(solution)/shard_map/slice | solution.py:58
  490.1 22.8 %collective-permute-done = bf16[512,2048]{1,0:T(8,128)(2,1)} collective-permute-done((bf16[512,2048]{1,0:T(8,128)(2,1)}, bf16[512,2048]{1,0:T(8,128)(2,1)}, u32[]{:S(2)}, u32[]{:S(2)}) %collective-permute-start) | collective-permute-done | bytes 2097184 | tf_op jit(solution)/shard_map/ppermute | solution.py:30
  512.9 44.0 %collective-permute-done.1 = bf16[512,2048]{1,0:T(8,128)(2,1)} collective-permute-done((bf16[512,2048]{1,0:T(8,128)(2,1)}, bf16[512,2048]{1,0:T(8,128)(2,1)}, u32[]{:S(2)}, u32[]{:S(2)}) %collective-permute-start.1) | collective-permute-done | bytes 2097184 | tf_op jit(solution)/shard_map/ppermute | solution.py:30
  583.0 15.5 slice_add_fusion.14
  598.5 15.5 slice_add_fusion.15
  615.2 31.5 %collective-permute-done.7 = bf16[512,2048]{1,0:T(8,128)(2,1)} collective-permute-done((bf16[512,2048]{1,0:T(8,128)(2,1)}, bf16[512,2048]{1,0:T(8,128)(2,1)}, u32[]{:S(2)}, u32[]{:S(2)}) %collective-permute-start.7) | collective-permute-done | bytes 2097184 | tf_op jit(solution)/shard_map/ppermute | solution.py:30
  651.7 14.6 slice_add_fusion.12
  675.4 14.6 slice_add_fusion.13
  692.6 43.9 %collective-permute-done.14 = bf16[512,2048]{1,0:T(8,128)(2,1)S(1)} collective-permute-done((bf16[512,2048]{1,0:T(8,128)(2,1)S(1)}, bf16[512,2048]{1,0:T(8,128)(2,1)S(1)}, u32[]{:S(2)}, u32[]{:S(2)}) %collective-permute-start.14) | collective-permute-done | bytes 2097184 | tf_op jit(solution)/shard_map/ppermute | solution.py:30
  739.6 14.5 slice_add_fusion.10
  754.0 14.5 slice_add_fusion.11
  768.5 13.9 collective-permute-done.15
  783.7 42.7 %collective-permute-done.17 = bf16[512,2048]{1,0:T(8,128)(2,1)S(1)} collective-permute-done((bf16[512,2048]{1,0:T(8,128)(2,1)S(1)}, bf16[512,2048]{1,0:T(8,128)(2,1)S(1)}, u32[]{:S(2)}, u32[]{:S(2)}) %collective-permute-start.17) | collective-permute-done | bytes 2097184 | tf_op jit(solution)/shard_map/ppermute | solution.py:30
  831.8 14.5 slice_add_fusion.8
  846.2 14.5 slice_add_fusion.9
  902.9 17.4 collective-permute-done.43
  935.2 74.0 %collective-permute-done.44 = f32[512,2048]{1,0:T(8,128)} collective-permute-done((f32[512,2048]{1,0:T(8,128)}, f32[512,2048]{1,0:T(8,128)}, u32[]{:S(2)}, u32[]{:S(2)}) %collective-permute-start.44) | collective-permute-done | bytes 4194336 | tf_op jit(solution)/shard_map/ppermute | solution.py:30
  1016.7 14.6 fusion.16
  1031.3 26.9 %collective-permute-done.19 = bf16[512,2048]{1,0:T(8,128)(2,1)S(1)} collective-permute-done((bf16[512,2048]{1,0:T(8,128)(2,1)S(1)}, bf16[512,2048]{1,0:T(8,128)(2,1)S(1)}, u32[]{:S(2)}, u32[]{:S(2)}) %collective-permute-start.19) | collective-permute-done | bytes 2097184 | tf_op jit(solution)/shard_map/ppermute | solution.py:30
  1058.1 42.6 %collective-permute-done.21 = bf16[512,2048]{1,0:T(8,128)(2,1)S(1)} collective-permute-done((bf16[512,2048]{1,0:T(8,128)(2,1)S(1)}, bf16[512,2048]{1,0:T(8,128)(2,1)S(1)}, u32[]{:S(2)}, u32[]{:S(2)}) %collective-permute-start.21) | collective-permute-done | bytes 2097184 | tf_op jit(solution)/shard_map/ppermute | solution.py:30
  1103.7 14.4 slice_add_fusion.6
  1131.7 14.6 slice_add_fusion.7
  1146.3 14.7 fusion.14
  1162.4 31.4 %collective-permute-done.25 = bf16[512,2048]{1,0:T(8,128)(2,1)S(1)} collective-permute-done((bf16[512,2048]{1,0:T(8,128)(2,1)S(1)}, bf16[512,2048]{1,0:T(8,128)(2,1)S(1)}, u32[]{:S(2)}, u32[]{:S(2)}) %collective-permute-start.25) | collective-permute-done | bytes 2097184 | tf_op jit(solution)/shard_map/ppermute | solution.py:30
  1198.5 15.9 slice_add_fusion.4
  1246.3 40.9 %collective-permute-done.45 = f32[512,2048]{1,0:T(8,128)} collective-permute-done((f32[512,2048]{1,0:T(8,128)}, f32[512,2048]{1,0:T(8,128)}, u32[]{:S(2)}, u32[]{:S(2)}) %collective-permute-start.45) | collective-permute-done | bytes 4194336 | tf_op jit(solution)/shard_map/ppermute | solution.py:30
  1306.0 71.0 %collective-permute-done.46 = f32[512,2048]{1,0:T(8,128)} collective-permute-done((f32[512,2048]{1,0:T(8,128)}, f32[512,2048]{1,0:T(8,128)}, u32[]{:S(2)}, u32[]{:S(2)}) %collective-permute-start.46) | collective-permute-done | bytes 4194336 | tf_op jit(solution)/shard_map/ppermute | solution.py:30
  1382.4 14.5 slice_add_fusion.5
  1396.9 14.9 fusion.12
  1430.7 14.4 slice_add_fusion.2
  1458.5 15.9 slice_add_fusion.3
  1478.4 14.6 fusion.10
  1493.0 21.1 %collective-permute-done.35 = bf16[512,2048]{1,0:T(8,128)(2,1)S(1)} collective-permute-done((bf16[512,2048]{1,0:T(8,128)(2,1)}, bf16[512,2048]{1,0:T(8,128)(2,1)S(1)}, u32[]{:S(2)}, u32[]{:S(2)}) %collective-permute-start.35) | collective-permute-done | bytes 2097184 | tf_op jit(solution)/shard_map/ppermute | solution.py:30
  1514.3 16.0 slice_add_fusion.1
  1589.3 14.6 fusion.8
  1617.7 14.6 fusion.6
  1645.7 14.9 fusion.4
  1687.8 47.2 %collective-permute-done.42 = f32[512,2048]{1,0:T(8,128)} collective-permute-done((f32[512,2048]{1,0:T(8,128)}, f32[512,2048]{1,0:T(8,128)}, u32[]{:S(2)}, u32[]{:S(2)}) %collective-permute-start.42) | collective-permute-done | bytes 4194336 | tf_op jit(solution)/shard_map/ppermute | solution.py:30
  (231 shorter events, 403.0 us)
Async XLA Ops:
  46.4 49.2 %collective-permute-start.3 = (bf16[4096,2048]{1,0:T(8,128)(2,1)}, bf16[4096,2048]{1,0:T(8,128)(2,1)S(1)}, u32[]{:S(2)}, u32[]{:S(2)}) collective-permute-start(bf16[4096,2048]{1,0:T(8,128)(2,1)} %bitcast.66), channel_id=1, source_target_pairs={{0,1},{1,0},{4,5},{5,4},{2,3},{3,2},{6,7},{7,6}} | collective-permute-start | bytes 50331656 | tf_op jit(solution)/shard_map/ppermute | solution.py:30
  47.3 48.4 %collective-permute-start.4 = (bf16[2048,2048]{1,0:T(8,128)(2,1)}, bf16[2048,2048]{1,0:T(8,128)(2,1)}, u32[]{:S(2)}, u32[]{:S(2)}) collective-permute-start(bf16[2048,2048]{1,0:T(8,128)(2,1)} %param.5), channel_id=1, source_target_pairs={{0,1},{1,0},{4,5},{5,4},{2,3},{3,2},{6,7},{7,6}} | collective-permute-start | bytes 25165832 | tf_op jit(solution)/shard_map/ppermute | solution.py:30
  47.3 183.9 %collective-permute-start.2 = (bf16[2048,2048]{1,0:T(8,128)(2,1)}, bf16[2048,2048]{1,0:T(8,128)(2,1)}, u32[]{:S(2)}, u32[]{:S(2)}) collective-permute-start(bf16[2048,2048]{1,0:T(8,128)(2,1)} %param.5), channel_id=1, source_target_pairs={{0,4},{1,5},{4,0},{5,1},{2,6},{3,7},{6,2},{7,3}} | collective-permute-start | bytes 25165832 | tf_op jit(solution)/shard_map/ppermute | solution.py:30
  50.3 182.4 %collective-permute-start.8 = (bf16[2048,2048]{1,0:T(8,128)(2,1)}, bf16[2048,2048]{1,0:T(8,128)(2,1)}, u32[]{:S(2)}, u32[]{:S(2)}) collective-permute-start(bf16[2048,2048]{1,0:T(8,128)(2,1)} %param.5), channel_id=1, source_target_pairs={{0,2},{1,3},{4,6},{5,7},{2,0},{3,1},{6,4},{7,5}} | collective-permute-start | bytes 25165832 | tf_op jit(solution)/shard_map/ppermute | solution.py:30
  231.2 27.7 %collective-permute-start.5 = (bf16[2048,2048]{1,0:T(8,128)(2,1)}, bf16[2048,2048]{1,0:T(8,128)(2,1)}, u32[]{:S(2)}, u32[]{:S(2)}) collective-permute-start(bf16[2048,2048]{1,0:T(8,128)(2,1)} %collective-permute-done.2), channel_id=1, source_target_pairs={{0,1},{1,0},{4,5},{5,4},{2,3},{3,2},{6,7},{7,6}} | collective-permute-start | bytes 25165832 | tf_op jit(solution)/shard_map/ppermute | solution.py:30
  232.7 69.7 %collective-permute-start.10 = (bf16[2048,2048]{1,0:T(8,128)(2,1)}, bf16[2048,2048]{1,0:T(8,128)(2,1)}, u32[]{:S(2)}, u32[]{:S(2)}) collective-permute-start(bf16[2048,2048]{1,0:T(8,128)(2,1)} %collective-permute-done.8), channel_id=1, source_target_pairs={{0,1},{1,0},{4,5},{5,4},{2,3},{3,2},{6,7},{7,6}} | collective-permute-start | bytes 25165832 | tf_op jit(solution)/shard_map/ppermute | solution.py:30
  240.9 185.1 %collective-permute-start.9 = (bf16[2048,2048]{1,0:T(8,128)(2,1)}, bf16[2048,2048]{1,0:T(8,128)(2,1)}, u32[]{:S(2)}, u32[]{:S(2)}) collective-permute-start(bf16[2048,2048]{1,0:T(8,128)(2,1)} %collective-permute-done.8), channel_id=1, source_target_pairs={{4,0},{5,1},{2,6},{3,7}} | collective-permute-start | bytes 25165832 | tf_op jit(solution)/shard_map/ppermute | solution.py:30
  426.0 147.3 %collective-permute-start.11 = (bf16[2048,2048]{1,0:T(8,128)(2,1)}, bf16[2048,2048]{1,0:T(8,128)(2,1)}, u32[]{:S(2)}, u32[]{:S(2)}) collective-permute-start(bf16[2048,2048]{1,0:T(8,128)(2,1)} %collective-permute-done.9), channel_id=1, source_target_pairs={{0,1},{1,0},{4,5},{5,4},{2,3},{3,2},{6,7},{7,6}} | collective-permute-start | bytes 25165832 | tf_op jit(solution)/shard_map/ppermute | solution.py:30
  464.0 48.8 %collective-permute-start = (bf16[512,2048]{1,0:T(8,128)(2,1)}, bf16[512,2048]{1,0:T(8,128)(2,1)}, u32[]{:S(2)}, u32[]{:S(2)}) collective-permute-start(bf16[512,2048]{1,0:T(8,128)(2,1)} %get-tuple-element.214), channel_id=1, source_target_pairs={{0,2},{1,3},{4,6},{5,7},{2,0},{3,1},{6,4},{7,5}} | collective-permute-start | bytes 6291464 | tf_op jit(solution)/shard_map/ppermute | solution.py:30
  486.1 70.8 %collective-permute-start.1 = (bf16[512,2048]{1,0:T(8,128)(2,1)}, bf16[512,2048]{1,0:T(8,128)(2,1)}, u32[]{:S(2)}, u32[]{:S(2)}) collective-permute-start(bf16[512,2048]{1,0:T(8,128)(2,1)} %get-tuple-element.202), channel_id=1, source_target_pairs={{0,2},{1,3},{4,7},{5,6},{2,1},{3,0},{6,4},{7,5}} | collective-permute-start | bytes 6291464 | tf_op jit(solution)/shard_map/ppermute | solution.py:30
  488.1 125.9 %collective-permute-start.6 = (bf16[512,2048]{1,0:T(8,128)(2,1)}, bf16[512,2048]{1,0:T(8,128)(2,1)}, u32[]{:S(2)}, u32[]{:S(2)}) collective-permute-start(bf16[512,2048]{1,0:T(8,128)(2,1)} %get-tuple-element.215), channel_id=1, source_target_pairs={{0,2},{1,3},{4,6},{5,7},{2,0},{3,1},{6,4},{7,5}} | collective-permute-start | bytes 6291464 | tf_op jit(solution)/shard_map/ppermute | solution.py:30
  488.2 158.5 %collective-permute-start.7 = (bf16[512,2048]{1,0:T(8,128)(2,1)}, bf16[512,2048]{1,0:T(8,128)(2,1)}, u32[]{:S(2)}, u32[]{:S(2)}) collective-permute-start(bf16[512,2048]{1,0:T(8,128)(2,1)} %get-tuple-element.203), channel_id=1, source_target_pairs={{0,2},{1,3},{4,7},{5,6},{2,1},{3,0},{6,4},{7,5}} | collective-permute-start | bytes 6291464 | tf_op jit(solution)/shard_map/ppermute | solution.py:30
  512.9 179.8 %collective-permute-start.12 = (bf16[512,2048]{1,0:T(8,128)(2,1)}, bf16[512,2048]{1,0:T(8,128)(2,1)}, u32[]{:S(2)}, u32[]{:S(2)}) collective-permute-start(bf16[512,2048]{1,0:T(8,128)(2,1)} %get-tuple-element.216), channel_id=1, source_target_pairs={{0,2},{1,3},{4,6},{5,7},{2,0},{3,1},{6,4},{7,5}} | collective-permute-start | bytes 6291464 | tf_op jit(solution)/shard_map/ppermute | solution.py:30
  556.9 109.5 %collective-permute-start.13 = (bf16[512,2048]{1,0:T(8,128)(2,1)}, bf16[512,2048]{1,0:T(8,128)(2,1)S(1)}, u32[]{:S(2)}, u32[]{:S(2)}) collective-permute-start(bf16[512,2048]{1,0:T(8,128)(2,1)} %get-tuple-element.116), channel_id=1, source_target_pairs={{4,0},{5,1},{2,6},{3,7}} | collective-permute-start | bytes 6291464 | tf_op jit(solution)/shard_map/ppermute | solution.py:30
  573.3 95.0 %collective-permute-start.16 = (bf16[512,2048]{1,0:T(8,128)(2,1)S(1)}, bf16[512,2048]{1,0:T(8,128)(2,1)}, u32[]{:S(2)}, u32[]{:S(2)}) collective-permute-start(bf16[512,2048]{1,0:T(8,128)(2,1)S(1)} %get-tuple-element.127), channel_id=1, source_target_pairs={{4,0},{5,1},{2,6},{3,7}} | collective-permute-start | bytes 6291464 | tf_op jit(solution)/shard_map/ppermute | solution.py:30
  614.0 251.0 %collective-permute-start.20 = (bf16[512,2048]{1,0:T(8,128)(2,1)}, bf16[512,2048]{1,0:T(8,128)(2,1)}, u32[]{:S(2)}, u32[]{:S(2)}) collective-permute-start(bf16[512,2048]{1,0:T(8,128)(2,1)} %get-tuple-element.138), channel_id=1, source_target_pairs={{4,0},{5,1},{2,6},{3,7}} | collective-permute-start | bytes 6291464 | tf_op jit(solution)/shard_map/ppermute | solution.py:30
  646.8 227.7 %collective-permute-start.24 = (bf16[512,2048]{1,0:T(8,128)(2,1)}, bf16[512,2048]{1,0:T(8,128)(2,1)}, u32[]{:S(2)}, u32[]{:S(2)}) collective-permute-start(bf16[512,2048]{1,0:T(8,128)(2,1)} %get-tuple-element.150), channel_id=1, source_target_pairs={{4,0},{5,1},{2,6},{3,7}} | collective-permute-start | bytes 6291464 | tf_op jit(solution)/shard_map/ppermute | solution.py:30
  666.4 555.6 %collective-permute-start.27 = (bf16[512,2048]{1,0:T(8,128)(2,1)}, bf16[512,2048]{1,0:T(8,128)(2,1)}, u32[]{:S(2)}, u32[]{:S(2)}) collective-permute-start(bf16[512,2048]{1,0:T(8,128)(2,1)} %get-tuple-element.162), channel_id=1, source_target_pairs={{4,0},{5,1},{2,6},{3,7}} | collective-permute-start | bytes 6291464 | tf_op jit(solution)/shard_map/ppermute | solution.py:30
  668.3 68.3 %collective-permute-start.14 = (bf16[512,2048]{1,0:T(8,128)(2,1)S(1)}, bf16[512,2048]{1,0:T(8,128)(2,1)S(1)}, u32[]{:S(2)}, u32[]{:S(2)}) collective-permute-start(bf16[512,2048]{1,0:T(8,128)(2,1)S(1)} %broadcast_select_fusion.24), channel_id=1, source_target_pairs={{0,2},{1,3},{4,7},{5,6},{2,1},{3,0},{6,4},{7,5}} | collective-permute-start | bytes 6291464 | tf_op jit(solution)/shard_map/ppermute | solution.py:30
  692.6 89.8 %collective-permute-start.15 = (bf16[512,2048]{1,0:T(8,128)(2,1)S(1)}, bf16[512,2048]{1,0:T(8,128)(2,1)S(1)}, u32[]{:S(2)}, u32[]{:S(2)}) collective-permute-start(bf16[512,2048]{1,0:T(8,128)(2,1)S(1)} %copy-done.31), channel_id=1, source_target_pairs={{0,2},{1,3},{4,6},{5,7},{2,0},{3,1},{6,4},{7,5}} | collective-permute-start | bytes 6291464 | tf_op jit(solution)/shard_map/ppermute | solution.py:30
  736.5 89.9 %collective-permute-start.17 = (bf16[512,2048]{1,0:T(8,128)(2,1)S(1)}, bf16[512,2048]{1,0:T(8,128)(2,1)S(1)}, u32[]{:S(2)}, u32[]{:S(2)}) collective-permute-start(bf16[512,2048]{1,0:T(8,128)(2,1)S(1)} %broadcast_select_fusion.23), channel_id=1, source_target_pairs={{0,2},{1,3},{4,7},{5,6},{2,1},{3,0},{6,4},{7,5}} | collective-permute-start | bytes 6291464 | tf_op jit(solution)/shard_map/ppermute | solution.py:30
  782.4 448.2 %collective-permute-start.29 = (bf16[512,2048]{1,0:T(8,128)(2,1)}, bf16[512,2048]{1,0:T(8,128)(2,1)}, u32[]{:S(2)}, u32[]{:S(2)}) collective-permute-start(bf16[512,2048]{1,0:T(8,128)(2,1)} %get-tuple-element.166), channel_id=1, source_target_pairs={{4,0},{5,1},{2,6},{3,7}} | collective-permute-start | bytes 6291464 | tf_op jit(solution)/shard_map/ppermute | solution.py:30
  826.4 93.9 %collective-permute-start.43 = (f32[512,2048]{1,0:T(8,128)}, f32[512,2048]{1,0:T(8,128)}, u32[]{:S(2)}, u32[]{:S(2)}) collective-permute-start(f32[512,2048]{1,0:T(8,128)} %slice_add_fusion.14), channel_id=1, source_target_pairs={{0,4},{1,5},{6,2},{7,3}} | collective-permute-start | bytes 12582920 | tf_op jit(solution)/shard_map/ppermute | solution.py:30
  864.9 144.2 %collective-permute-start.44 = (f32[512,2048]{1,0:T(8,128)}, f32[512,2048]{1,0:T(8,128)}, u32[]{:S(2)}, u32[]{:S(2)}) collective-permute-start(f32[512,2048]{1,0:T(8,128)} %slice_add_fusion.12), channel_id=1, source_target_pairs={{0,4},{1,5},{6,2},{7,3}} | collective-permute-start | bytes 12582920 | tf_op jit(solution)/shard_map/ppermute | solution.py:30
  874.4 140.0 %collective-permute-start.18 = (bf16[512,4096]{1,0:T(8,128)(2,1)}, bf16[512,4096]{1,0:T(8,128)(2,1)}, u32[]{:S(2)}, u32[]{:S(2)}) collective-permute-start(bf16[512,4096]{1,0:T(8,128)(2,1)} %pad_maximum_fusion), channel_id=1, source_target_pairs={{0,1},{1,0},{4,5},{5,4},{2,3},{3,2},{6,7},{7,6}} | collective-permute-start | bytes 12582920 | tf_op jit(solution)/shard_map/ppermute | solution.py:30
  920.3 317.2 %collective-permute-start.32 = (bf16[512,2048]{1,0:T(8,128)(2,1)}, bf16[512,2048]{1,0:T(8,128)(2,1)}, u32[]{:S(2)}, u32[]{:S(2)}) collective-permute-start(bf16[512,2048]{1,0:T(8,128)(2,1)} %get-tuple-element.172), channel_id=1, source_target_pairs={{4,0},{5,1},{2,6},{3,7}} | collective-permute-start | bytes 6291464 | tf_op jit(solution)/shard_map/ppermute | solution.py:30
  1009.2 49.0 %collective-permute-start.19 = (bf16[512,2048]{1,0:T(8,128)(2,1)S(1)}, bf16[512,2048]{1,0:T(8,128)(2,1)S(1)}, u32[]{:S(2)}, u32[]{:S(2)}) collective-permute-start(bf16[512,2048]{1,0:T(8,128)(2,1)S(1)} %copy-done.30), channel_id=1, source_target_pairs={{0,2},{1,3},{4,6},{5,7},{2,0},{3,1},{6,4},{7,5}} | collective-permute-start | bytes 6291464 | tf_op jit(solution)/shard_map/ppermute | solution.py:30
  1014.5 86.3 %collective-permute-start.21 = (bf16[512,2048]{1,0:T(8,128)(2,1)S(1)}, bf16[512,2048]{1,0:T(8,128)(2,1)S(1)}, u32[]{:S(2)}, u32[]{:S(2)}) collective-permute-start(bf16[512,2048]{1,0:T(8,128)(2,1)S(1)} %copy-done.34), channel_id=1, source_target_pairs={{0,2},{1,3},{4,7},{5,6},{2,1},{3,0},{6,4},{7,5}} | collective-permute-start | bytes 6291464 | tf_op jit(solution)/shard_map/ppermute | solution.py:30
  1058.1 88.1 %collective-permute-start.22 = (bf16[512,4096]{1,0:T(8,128)(2,1)S(1)}, bf16[512,4096]{1,0:T(8,128)(2,1)}, u32[]{:S(2)}, u32[]{:S(2)}) collective-permute-start(bf16[512,4096]{1,0:T(8,128)(2,1)S(1)} %pad_maximum_fusion.1), channel_id=1, source_target_pairs={{0,1},{1,0},{4,5},{5,4},{2,3},{3,2},{6,7},{7,6}} | collective-permute-start | bytes 12582920 | tf_op jit(solution)/shard_map/ppermute | solution.py:30
  1100.7 60.3 %collective-permute-start.23 = (bf16[512,2048]{1,0:T(8,128)(2,1)S(1)}, bf16[512,2048]{1,0:T(8,128)(2,1)S(1)}, u32[]{:S(2)}, u32[]{:S(2)}) collective-permute-start(bf16[512,2048]{1,0:T(8,128)(2,1)S(1)} %copy-done.29), channel_id=1, source_target_pairs={{0,2},{1,3},{4,6},{5,7},{2,0},{3,1},{6,4},{7,5}} | collective-permute-start | bytes 6291464 | tf_op jit(solution)/shard_map/ppermute | solution.py:30
  1146.3 47.5 %collective-permute-start.25 = (bf16[512,2048]{1,0:T(8,128)(2,1)S(1)}, bf16[512,2048]{1,0:T(8,128)(2,1)S(1)}, u32[]{:S(2)}, u32[]{:S(2)}) collective-permute-start(bf16[512,2048]{1,0:T(8,128)(2,1)S(1)} %copy-done.32), channel_id=1, source_target_pairs={{0,2},{1,3},{4,7},{5,6},{2,1},{3,0},{6,4},{7,5}} | collective-permute-start | bytes 6291464 | tf_op jit(solution)/shard_map/ppermute | solution.py:30
  1161.1 83.1 %collective-permute-start.34 = (bf16[512,2048]{1,0:T(8,128)(2,1)S(1)}, bf16[512,2048]{1,0:T(8,128)(2,1)S(1)}, u32[]{:S(2)}, u32[]{:S(2)}) collective-permute-start(bf16[512,2048]{1,0:T(8,128)(2,1)S(1)} %copy-done), channel_id=1, source_target_pairs={{4,0},{5,1},{2,6},{3,7}} | collective-permute-start | bytes 6291464 | tf_op jit(solution)/shard_map/ppermute | solution.py:30
  1193.8 93.4 %collective-permute-start.45 = (f32[512,2048]{1,0:T(8,128)}, f32[512,2048]{1,0:T(8,128)}, u32[]{:S(2)}, u32[]{:S(2)}) collective-permute-start(f32[512,2048]{1,0:T(8,128)} %slice_add_fusion.10), channel_id=1, source_target_pairs={{0,4},{1,5},{6,2},{7,3}} | collective-permute-start | bytes 12582920 | tf_op jit(solution)/shard_map/ppermute | solution.py:30
  1221.9 155.1 %collective-permute-start.46 = (f32[512,2048]{1,0:T(8,128)}, f32[512,2048]{1,0:T(8,128)}, u32[]{:S(2)}, u32[]{:S(2)}) collective-permute-start(f32[512,2048]{1,0:T(8,128)} %slice_add_fusion.8), channel_id=1, source_target_pairs={{0,4},{1,5},{6,2},{7,3}} | collective-permute-start | bytes 12582920 | tf_op jit(solution)/shard_map/ppermute | solution.py:30
  1230.6 457.2 %collective-permute-start.40 = (f32[512,2048]{1,0:T(8,128)}, f32[512,2048]{1,0:T(8,128)}, u32[]{:S(2)}, u32[]{:S(2)}) collective-permute-start(f32[512,2048]{1,0:T(8,128)} %slice_add_fusion.4), channel_id=1, source_target_pairs={{0,4},{1,5},{6,2},{7,3}} | collective-permute-start | bytes 12582920 | tf_op jit(solution)/shard_map/ppermute | solution.py:30
  1237.5 330.7 %collective-permute-start.47 = (f32[512,2048]{1,0:T(8,128)}, f32[512,2048]{1,0:T(8,128)}, u32[]{:S(2)}, u32[]{:S(2)}) collective-permute-start(f32[512,2048]{1,0:T(8,128)} %slice_add_fusion.6), channel_id=1, source_target_pairs={{0,4},{1,5},{6,2},{7,3}} | collective-permute-start | bytes 12582920 | tf_op jit(solution)/shard_map/ppermute | solution.py:30
  1244.2 152.7 %collective-permute-start.26 = (bf16[512,4096]{1,0:T(8,128)(2,1)}, bf16[512,4096]{1,0:T(8,128)(2,1)}, u32[]{:S(2)}, u32[]{:S(2)}) collective-permute-start(bf16[512,4096]{1,0:T(8,128)(2,1)} %pad_maximum_fusion.2), channel_id=1, source_target_pairs={{0,1},{1,0},{4,5},{5,4},{2,3},{3,2},{6,7},{7,6}} | collective-permute-start | bytes 12582920 | tf_op jit(solution)/shard_map/ppermute | solution.py:30
  1287.2 124.6 %collective-permute-start.28 = (bf16[512,2048]{1,0:T(8,128)(2,1)}, bf16[512,2048]{1,0:T(8,128)(2,1)S(1)}, u32[]{:S(2)}, u32[]{:S(2)}) collective-permute-start(bf16[512,2048]{1,0:T(8,128)(2,1)} %broadcast_select_fusion.14), channel_id=1, source_target_pairs={{0,2},{1,3},{4,6},{5,7},{2,0},{3,1},{6,4},{7,5}} | collective-permute-start | bytes 6291464 | tf_op jit(solution)/shard_map/ppermute | solution.py:30
  1377.1 48.8 %collective-permute-start.30 = (bf16[512,2048]{1,0:T(8,128)(2,1)}, bf16[512,2048]{1,0:T(8,128)(2,1)S(1)}, u32[]{:S(2)}, u32[]{:S(2)}) collective-permute-start(bf16[512,2048]{1,0:T(8,128)(2,1)} %broadcast_select_fusion.13), channel_id=1, source_target_pairs={{0,2},{1,3},{4,7},{5,6},{2,1},{3,0},{6,4},{7,5}} | collective-permute-start | bytes 6291464 | tf_op jit(solution)/shard_map/ppermute | solution.py:30
  1396.8 77.5 %collective-permute-start.31 = (bf16[512,4096]{1,0:T(8,128)(2,1)S(1)}, bf16[512,4096]{1,0:T(8,128)(2,1)}, u32[]{:S(2)}, u32[]{:S(2)}) collective-permute-start(bf16[512,4096]{1,0:T(8,128)(2,1)S(1)} %pad_maximum_fusion.3), channel_id=1, source_target_pairs={{0,1},{1,0},{4,5},{5,4},{2,3},{3,2},{6,7},{7,6}} | collective-permute-start | bytes 12582920 | tf_op jit(solution)/shard_map/ppermute | solution.py:30
  1411.8 81.2 %collective-permute-start.33 = (bf16[512,2048]{1,0:T(8,128)(2,1)S(1)}, bf16[512,2048]{1,0:T(8,128)(2,1)S(1)}, u32[]{:S(2)}, u32[]{:S(2)}) collective-permute-start(bf16[512,2048]{1,0:T(8,128)(2,1)S(1)} %copy-done.33), channel_id=1, source_target_pairs={{0,2},{1,3},{4,6},{5,7},{2,0},{3,1},{6,4},{7,5}} | collective-permute-start | bytes 6291464 | tf_op jit(solution)/shard_map/ppermute | solution.py:30
  1425.9 88.1 %collective-permute-start.35 = (bf16[512,2048]{1,0:T(8,128)(2,1)}, bf16[512,2048]{1,0:T(8,128)(2,1)S(1)}, u32[]{:S(2)}, u32[]{:S(2)}) collective-permute-start(bf16[512,2048]{1,0:T(8,128)(2,1)} %broadcast_select_fusion.9), channel_id=1, source_target_pairs={{0,2},{1,3},{4,7},{5,6},{2,1},{3,0},{6,4},{7,5}} | collective-permute-start | bytes 6291464 | tf_op jit(solution)/shard_map/ppermute | solution.py:30
  1474.4 213.4 %collective-permute-start.41 = (f32[512,2048]{1,0:T(8,128)}, f32[512,2048]{1,0:T(8,128)}, u32[]{:S(2)}, u32[]{:S(2)}) collective-permute-start(f32[512,2048]{1,0:T(8,128)} %slice_add_fusion.2), channel_id=1, source_target_pairs={{0,4},{1,5},{6,2},{7,3}} | collective-permute-start | bytes 12582920 | tf_op jit(solution)/shard_map/ppermute | solution.py:30
  1530.3 204.7 %collective-permute-start.42 = (f32[512,2048]{1,0:T(8,128)}, f32[512,2048]{1,0:T(8,128)}, u32[]{:S(2)}, u32[]{:S(2)}) collective-permute-start(f32[512,2048]{1,0:T(8,128)} %slice_add_fusion.1), channel_id=1, source_target_pairs={{0,4},{1,5},{6,2},{7,3}} | collective-permute-start | bytes 12582920 | tf_op jit(solution)/shard_map/ppermute | solution.py:30
  1540.8 48.1 %collective-permute-start.36 = (bf16[512,4096]{1,0:T(8,128)(2,1)}, bf16[512,4096]{1,0:T(8,128)(2,1)}, u32[]{:S(2)}, u32[]{:S(2)}) collective-permute-start(bf16[512,4096]{1,0:T(8,128)(2,1)} %pad_maximum_fusion.4), channel_id=1, source_target_pairs={{0,1},{1,0},{4,5},{5,4},{2,3},{3,2},{6,7},{7,6}} | collective-permute-start | bytes 12582920 | tf_op jit(solution)/shard_map/ppermute | solution.py:30
  1568.2 49.2 %collective-permute-start.37 = (bf16[512,4096]{1,0:T(8,128)(2,1)}, bf16[512,4096]{1,0:T(8,128)(2,1)}, u32[]{:S(2)}, u32[]{:S(2)}) collective-permute-start(bf16[512,4096]{1,0:T(8,128)(2,1)} %pad_maximum_fusion.5), channel_id=1, source_target_pairs={{0,1},{1,0},{4,5},{5,4},{2,3},{3,2},{6,7},{7,6}} | collective-permute-start | bytes 12582920 | tf_op jit(solution)/shard_map/ppermute | solution.py:30
  1589.0 56.7 %collective-permute-start.38 = (bf16[512,4096]{1,0:T(8,128)(2,1)}, bf16[512,4096]{1,0:T(8,128)(2,1)}, u32[]{:S(2)}, u32[]{:S(2)}) collective-permute-start(bf16[512,4096]{1,0:T(8,128)(2,1)} %pad_maximum_fusion.6), channel_id=1, source_target_pairs={{0,1},{1,0},{4,5},{5,4},{2,3},{3,2},{6,7},{7,6}} | collective-permute-start | bytes 12582920 | tf_op jit(solution)/shard_map/ppermute | solution.py:30
  1617.5 56.5 %collective-permute-start.39 = (bf16[512,4096]{1,0:T(8,128)(2,1)}, bf16[512,4096]{1,0:T(8,128)(2,1)S(1)}, u32[]{:S(2)}, u32[]{:S(2)}) collective-permute-start(bf16[512,4096]{1,0:T(8,128)(2,1)} %pad_maximum_fusion.7), channel_id=1, source_target_pairs={{0,1},{1,0},{4,5},{5,4},{2,3},{3,2},{6,7},{7,6}} | collective-permute-start | bytes 12582920 | tf_op jit(solution)/shard_map/ppermute | solution.py:30
  (41 other events, 1140.9 us)

commit v3 on v2

--- a/solution.py
+++ b/solution.py
@@ -64,8 +64,9 @@
         x_same = lax.dynamic_slice(act_blk, (0, core * feats), (tokens, feats)).T
         x_other = lax.dynamic_slice(act_blk, (0, (1 - core) * feats), (tokens, feats)).T
         x_q = _send(x_other, Q_SWAP)
-        near_own = _mm(x_same, grad_blk) + _mm(x_q, g_q)
+        near_own = _mm(x_same, grad_blk)
         g_x, g_y = _tie(g_x, near_own), _tie(g_y, near_own)
+        near_own = near_own + _mm(x_q, g_q)
         g_d = _send(g_x, Y_TO_DIAG)
 
         w_y = [_send(_tie(cut(w_blk, j), g_x), Y_TO_DIAG) for j in range(CHUNKS)]
@@ -90,7 +91,7 @@
         g_xx = jnp.concatenate([g_x, _send(g_x, Q_SWAP)], axis=0)
         far_own = _mm(x_same, g_y) + _mm(x_q, g_yq)
         g_all = jnp.concatenate([grad_blk, g_y], axis=1)
-        g_d = _tie(g_d, far_own, g_xx, g_all)
+        g_d = _tie(g_d, far_own, near_own, g_xx, g_all)
         g_dd = jnp.concatenate([g_d, _send(g_d, Q_SWAP)], axis=0)
 
         def put(out, j, both):

time: 1760 us -> 1750 us (level)
    unnamed x95 -> x93, local copies, waits for them, and re-layouts: 87.4 us -> 86.8 us
  transfers between devices with their start and end apart: 48 -> 48, of which waited for: 20 -> 20; matrix products, arithmetic and copies ran while one was open for 49% -> 52% of each run, Pallas kernels for 0% -> 0%
where the time goes in v3:
time: 1750 us; the launch traced here: 1740 us
  waiting for transfers between devices  737 us (42%)
  matrix products  640 us (37%)
  local copies, waits for them, and re-layouts  165 us (9%)
  other arithmetic  116 us (7%)
  starting transfers between devices  77.4 us (4%)
    ppermute x48, waiting for transfers between devices, _send(): return lax.ppermute(value, AXES, pairs)  737 us
    dot_general x36, matrix products, _mm(): lax.dot_general(a, b, (((1,), (over,)), ((), ())), preferred_element_type...  640 us
    unnamed x93, local copies, waits for them, and re-layouts  86.8 us
    ppermute x48, starting transfers between devices, _send(): return lax.ppermute(value, AXES, pairs)  77.4 us
    slice x2, other arithmetic, cut(): return a[j * width:(j + 1) * width]  37.6 us
  transfers between devices with their start and end apart: 48, of which 20 were waited for; matrix products, arithmetic and copies ran while one was open for 52% of the time, Pallas kernels for 0%

profile of v3, /device:TPU:0, one launch (start us, length us, event | category | flops | bytes accessed | tf_op | source)
XLA Modules:
  0.0 1737.0 jit_solution(13974069006228530453)
XLA Ops:
  4.0 23.2 %constant_dynamic-slice_fusion = (bf16[2048,4096]{1,0:T(8,128)(2,1)}, bf16[2048,4096]{1,0:T(8,128)(2,1)}) fusion(bf16[2048,8192]{1,0:T(8,128)(2,1)} %param.3, s32[]{:T(128)S(6)} %select_n.232, s32[]{:T(128)S(6)} %select_n.230), kind=kLoop, calls=%fused_computation.121 | loop fusion | bytes 67108872 | tf_op jit(solution)/shard_map/dynamic_slice | solution.py:65
  27.2 21.8 %copy.8 = bf16[2048,4096]{0,1:T(8,128)(2,1)} copy(bf16[2048,4096]{1,0:T(8,128)(2,1)} %get-tuple-element.194) | data formatting | bytes 33554432
  50.5 43.9 %fusion.20 = f32[4096,2048]{1,0:T(8,128)} fusion(bf16[2048,4096]{1,0:T(8,128)(2,1)} %get-tuple-element.195, bf16[2048,2048]{1,0:T(8,128)(2,1)} %param.5), kind=kOutput, calls=%fused_computation.125 | convolution fusion | flops 34359738368 | bytes 58720256 | tf_op jit(solution)/shard_map/dot_general | solution.py:41
  94.4 90.3 %collective-permute-done.2 = bf16[2048,2048]{1,0:T(8,128)(2,1)} collective-permute-done((bf16[2048,2048]{1,0:T(8,128)(2,1)}, bf16[2048,2048]{1,0:T(8,128)(2,1)}, u32[]{:S(2)}, u32[]{:S(2)}) %collective-permute-start.2) | collective-permute-done | bytes 8388640 | tf_op jit(solution)/shard_map/ppermute | solution.py:30
  193.7 38.5 %collective-permute-done.8 = bf16[2048,2048]{1,0:T(8,128)(2,1)} collective-permute-done((bf16[2048,2048]{1,0:T(8,128)(2,1)}, bf16[2048,2048]{1,0:T(8,128)(2,1)}, u32[]{:S(2)}, u32[]{:S(2)}) %collective-permute-start.8) | collective-permute-done | bytes 8388640 | tf_op jit(solution)/shard_map/ppermute | solution.py:30
  250.9 43.3 %fusion.21 = f32[4096,2048]{1,0:T(8,128)} fusion(bf16[4096,2048]{1,0:T(8,128)(2,1)} %collective-permute-done.3, bf16[2048,2048]{1,0:T(8,128)(2,1)} %collective-permute-done.4), kind=kOutput, calls=%fused_computation.126 | convolution fusion | flops 34359738368 | bytes 58720256 | tf_op jit(solution)/shard_map/dot_general | solution.py:41
  294.2 46.3 %convolution_add_fusion.1 = f32[4096,2048]{1,0:T(8,128)} fusion(f32[4096,2048]{1,0:T(8,128)} %fusion.21, bf16[2048,4096]{1,0:T(8,128)(2,1)} %get-tuple-element.195, bf16[2048,2048]{1,0:T(8,128)(2,1)} %collective-permute-done.2), kind=kOutput, calls=%fused_computation.1 | convolution fusion | flops 34368126976 | bytes 92274688 | tf_op jit(solution)/shard_map/dot_general | solution.py:41
  348.8 44.4 %convolution_add_fusion = f32[4096,2048]{1,0:T(8,128)} fusion(f32[4096,2048]{1,0:T(8,128)} %fusion.20, bf16[4096,2048]{1,0:T(8,128)(2,1)} %collective-permute-done.3, bf16[2048,2048]{1,0:T(8,128)(2,1)} %collective-permute-done.7), kind=kOutput, calls=%fused_computation | convolution fusion | flops 34368126976 | bytes 92274688 | tf_op jit(solution)/shard_map/dot_general | solution.py:41
  393.2 23.2 %collective-permute-done.9 = bf16[2048,2048]{1,0:T(8,128)(2,1)} collective-permute-done((bf16[2048,2048]{1,0:T(8,128)(2,1)}, bf16[2048,2048]{1,0:T(8,128)(2,1)}, u32[]{:S(2)}, u32[]{:S(2)}) %collective-permute-start.9) | collective-permute-done | bytes 8388640 | tf_op jit(solution)/shard_map/ppermute | solution.py:30
  416.4 22.4 %copy.7 = bf16[2048,4096]{0,1:T(8,128)(2,1)} copy(bf16[2048,4096]{1,0:T(8,128)(2,1)} %get-tuple-element.195) | data formatting | bytes 33554432
  438.9 15.6 fusion.19
  454.5 22.0 %fusion.18 = (bf16[512,2048]{1,0:T(8,128)(2,1)}, bf16[512,2048]{1,0:T(8,128)(2,1)}, bf16[512,2048]{1,0:T(8,128)(2,1)}, bf16[512,2048]{1,0:T(8,128)(2,1)}, bf16[5...) fusion(bf16[4096,2048]{1,0:T(8,128)(2,1)} %bitcast.67, ...), kind=kLoop, calls=%fused_computation.123 | loop fusion | flops 2097152 | bytes 67108864 | tf_op jit(solution)/shard_map/slice | solution.py:58
  480.6 22.8 %collective-permute-done = bf16[512,2048]{1,0:T(8,128)(2,1)} collective-permute-done((bf16[512,2048]{1,0:T(8,128)(2,1)}, bf16[512,2048]{1,0:T(8,128)(2,1)}, u32[]{:S(2)}, u32[]{:S(2)}) %collective-permute-start) | collective-permute-done | bytes 2097184 | tf_op jit(solution)/shard_map/ppermute | solution.py:30
  503.3 44.0 %collective-permute-done.1 = bf16[512,2048]{1,0:T(8,128)(2,1)} collective-permute-done((bf16[512,2048]{1,0:T(8,128)(2,1)}, bf16[512,2048]{1,0:T(8,128)(2,1)}, u32[]{:S(2)}, u32[]{:S(2)}) %collective-permute-start.1) | collective-permute-done | bytes 2097184 | tf_op jit(solution)/shard_map/ppermute | solution.py:30
  573.0 16.0 slice_add_fusion.14
  589.0 15.6 slice_add_fusion.15
  605.9 31.3 %collective-permute-done.6 = bf16[512,2048]{1,0:T(8,128)(2,1)} collective-permute-done((bf16[512,2048]{1,0:T(8,128)(2,1)}, bf16[512,2048]{1,0:T(8,128)(2,1)}, u32[]{:S(2)}, u32[]{:S(2)}) %collective-permute-start.6) | collective-permute-done | bytes 2097184 | tf_op jit(solution)/shard_map/ppermute | solution.py:30
  642.2 14.7 slice_add_fusion.12
  665.8 14.8 slice_add_fusion.13
  683.1 43.9 %collective-permute-done.14 = bf16[512,2048]{1,0:T(8,128)(2,1)S(1)} collective-permute-done((bf16[512,2048]{1,0:T(8,128)(2,1)S(1)}, bf16[512,2048]{1,0:T(8,128)(2,1)S(1)}, u32[]{:S(2)}, u32[]{:S(2)}) %collective-permute-start.14) | collective-permute-done | bytes 2097184 | tf_op jit(solution)/shard_map/ppermute | solution.py:30
  730.0 14.6 slice_add_fusion.10
  744.6 14.5 slice_add_fusion.11
  774.2 42.7 %collective-permute-done.17 = bf16[512,2048]{1,0:T(8,128)(2,1)S(1)} collective-permute-done((bf16[512,2048]{1,0:T(8,128)(2,1)S(1)}, bf16[512,2048]{1,0:T(8,128)(2,1)S(1)}, u32[]{:S(2)}, u32[]{:S(2)}) %collective-permute-start.17) | collective-permute-done | bytes 2097184 | tf_op jit(solution)/shard_map/ppermute | solution.py:30
  822.0 14.8 slice_add_fusion.8
  836.8 14.6 slice_add_fusion.9
  893.6 17.2 collective-permute-done.43
  925.1 74.5 %collective-permute-done.44 = f32[512,2048]{1,0:T(8,128)} collective-permute-done((f32[512,2048]{1,0:T(8,128)}, f32[512,2048]{1,0:T(8,128)}, u32[]{:S(2)}, u32[]{:S(2)}) %collective-permute-start.44) | collective-permute-done | bytes 4194336 | tf_op jit(solution)/shard_map/ppermute | solution.py:30
  1007.1 14.6 fusion.16
  1021.7 26.9 %collective-permute-done.19 = bf16[512,2048]{1,0:T(8,128)(2,1)S(1)} collective-permute-done((bf16[512,2048]{1,0:T(8,128)(2,1)S(1)}, bf16[512,2048]{1,0:T(8,128)(2,1)S(1)}, u32[]{:S(2)}, u32[]{:S(2)}) %collective-permute-start.19) | collective-permute-done | bytes 2097184 | tf_op jit(solution)/shard_map/ppermute | solution.py:30
  1048.6 42.6 %collective-permute-done.21 = bf16[512,2048]{1,0:T(8,128)(2,1)S(1)} collective-permute-done((bf16[512,2048]{1,0:T(8,128)(2,1)S(1)}, bf16[512,2048]{1,0:T(8,128)(2,1)S(1)}, u32[]{:S(2)}, u32[]{:S(2)}) %collective-permute-start.21) | collective-permute-done | bytes 2097184 | tf_op jit(solution)/shard_map/ppermute | solution.py:30
  1094.2 14.5 slice_add_fusion.6
  1122.2 14.7 slice_add_fusion.7
  1136.9 14.7 fusion.14
  1153.0 31.2 %collective-permute-done.25 = bf16[512,2048]{1,0:T(8,128)(2,1)S(1)} collective-permute-done((bf16[512,2048]{1,0:T(8,128)(2,1)S(1)}, bf16[512,2048]{1,0:T(8,128)(2,1)S(1)}, u32[]{:S(2)}, u32[]{:S(2)}) %collective-permute-start.25) | collective-permute-done | bytes 2097184 | tf_op jit(solution)/shard_map/ppermute | solution.py:30
  1189.0 16.0 slice_add_fusion.4
  1236.9 40.7 %collective-permute-done.45 = f32[512,2048]{1,0:T(8,128)} collective-permute-done((f32[512,2048]{1,0:T(8,128)}, f32[512,2048]{1,0:T(8,128)}, u32[]{:S(2)}, u32[]{:S(2)}) %collective-permute-start.45) | collective-permute-done | bytes 4194336 | tf_op jit(solution)/shard_map/ppermute | solution.py:30
  1296.5 71.0 %collective-permute-done.46 = f32[512,2048]{1,0:T(8,128)} collective-permute-done((f32[512,2048]{1,0:T(8,128)}, f32[512,2048]{1,0:T(8,128)}, u32[]{:S(2)}, u32[]{:S(2)}) %collective-permute-start.46) | collective-permute-done | bytes 4194336 | tf_op jit(solution)/shard_map/ppermute | solution.py:30
  1372.8 14.5 slice_add_fusion.5
  1387.4 14.9 fusion.12
  1421.1 14.5 slice_add_fusion.2
  1449.0 15.8 slice_add_fusion.3
  1468.7 14.7 fusion.10
  1483.5 21.0 %collective-permute-done.35 = bf16[512,2048]{1,0:T(8,128)(2,1)S(1)} collective-permute-done((bf16[512,2048]{1,0:T(8,128)(2,1)}, bf16[512,2048]{1,0:T(8,128)(2,1)S(1)}, u32[]{:S(2)}, u32[]{:S(2)}) %collective-permute-start.35) | collective-permute-done | bytes 2097184 | tf_op jit(solution)/shard_map/ppermute | solution.py:30
  1504.8 16.1 slice_add_fusion.1
  1579.9 14.6 fusion.8
  1608.2 14.6 fusion.6
  1636.3 14.8 fusion.4
  1678.3 47.1 %collective-permute-done.42 = f32[512,2048]{1,0:T(8,128)} collective-permute-done((f32[512,2048]{1,0:T(8,128)}, f32[512,2048]{1,0:T(8,128)}, u32[]{:S(2)}, u32[]{:S(2)}) %collective-permute-start.42) | collective-permute-done | bytes 4194336 | tf_op jit(solution)/shard_map/ppermute | solution.py:30
  (229 shorter events, 414.6 us)
Async XLA Ops:
  0.6 184.1 %collective-permute-start.2 = (bf16[2048,2048]{1,0:T(8,128)(2,1)}, bf16[2048,2048]{1,0:T(8,128)(2,1)}, u32[]{:S(2)}, u32[]{:S(2)}) collective-permute-start(bf16[2048,2048]{1,0:T(8,128)(2,1)} %param.5), channel_id=1, source_target_pairs={{0,4},{1,5},{4,0},{5,1},{2,6},{3,7},{6,2},{7,3}} | collective-permute-start | bytes 25165832 | tf_op jit(solution)/shard_map/ppermute | solution.py:30
  49.0 201.8 %collective-permute-start.3 = (bf16[4096,2048]{1,0:T(8,128)(2,1)}, bf16[4096,2048]{1,0:T(8,128)(2,1)}, u32[]{:S(2)}, u32[]{:S(2)}) collective-permute-start(bf16[4096,2048]{1,0:T(8,128)(2,1)} %bitcast.66), channel_id=1, source_target_pairs={{0,1},{1,0},{4,5},{5,4},{2,3},{3,2},{6,7},{7,6}} | collective-permute-start | bytes 50331656 | tf_op jit(solution)/shard_map/ppermute | solution.py:30
  49.0 183.2 %collective-permute-start.8 = (bf16[2048,2048]{1,0:T(8,128)(2,1)}, bf16[2048,2048]{1,0:T(8,128)(2,1)}, u32[]{:S(2)}, u32[]{:S(2)}) collective-permute-start(bf16[2048,2048]{1,0:T(8,128)(2,1)} %param.5), channel_id=1, source_target_pairs={{0,2},{1,3},{4,6},{5,7},{2,0},{3,1},{6,4},{7,5}} | collective-permute-start | bytes 25165832 | tf_op jit(solution)/shard_map/ppermute | solution.py:30
  184.8 66.1 %collective-permute-start.4 = (bf16[2048,2048]{1,0:T(8,128)(2,1)}, bf16[2048,2048]{1,0:T(8,128)(2,1)}, u32[]{:S(2)}, u32[]{:S(2)}) collective-permute-start(bf16[2048,2048]{1,0:T(8,128)(2,1)} %collective-permute-done.2), channel_id=1, source_target_pairs={{0,1},{1,0},{4,5},{5,4},{2,3},{3,2},{6,7},{7,6}} | collective-permute-start | bytes 25165832 | tf_op jit(solution)/shard_map/ppermute | solution.py:30
  184.8 164.1 %collective-permute-start.7 = (bf16[2048,2048]{1,0:T(8,128)(2,1)}, bf16[2048,2048]{1,0:T(8,128)(2,1)}, u32[]{:S(2)}, u32[]{:S(2)}) collective-permute-start(bf16[2048,2048]{1,0:T(8,128)(2,1)} %param.5), channel_id=1, source_target_pairs={{0,1},{1,0},{4,5},{5,4},{2,3},{3,2},{6,7},{7,6}} | collective-permute-start | bytes 25165832 | tf_op jit(solution)/shard_map/ppermute | solution.py:30
  232.2 184.2 %collective-permute-start.9 = (bf16[2048,2048]{1,0:T(8,128)(2,1)}, bf16[2048,2048]{1,0:T(8,128)(2,1)}, u32[]{:S(2)}, u32[]{:S(2)}) collective-permute-start(bf16[2048,2048]{1,0:T(8,128)(2,1)} %collective-permute-done.8), channel_id=1, source_target_pairs={{4,0},{5,1},{2,6},{3,7}} | collective-permute-start | bytes 25165832 | tf_op jit(solution)/shard_map/ppermute | solution.py:30
  234.0 106.5 %collective-permute-start.10 = (bf16[2048,2048]{1,0:T(8,128)(2,1)}, bf16[2048,2048]{1,0:T(8,128)(2,1)}, u32[]{:S(2)}, u32[]{:S(2)}) collective-permute-start(bf16[2048,2048]{1,0:T(8,128)(2,1)} %collective-permute-done.8), channel_id=1, source_target_pairs={{0,1},{1,0},{4,5},{5,4},{2,3},{3,2},{6,7},{7,6}} | collective-permute-start | bytes 25165832 | tf_op jit(solution)/shard_map/ppermute | solution.py:30
  416.4 146.9 %collective-permute-start.11 = (bf16[2048,2048]{1,0:T(8,128)(2,1)}, bf16[2048,2048]{1,0:T(8,128)(2,1)}, u32[]{:S(2)}, u32[]{:S(2)}) collective-permute-start(bf16[2048,2048]{1,0:T(8,128)(2,1)} %collective-permute-done.9), channel_id=1, source_target_pairs={{0,1},{1,0},{4,5},{5,4},{2,3},{3,2},{6,7},{7,6}} | collective-permute-start | bytes 25165832 | tf_op jit(solution)/shard_map/ppermute | solution.py:30
  454.5 48.8 %collective-permute-start = (bf16[512,2048]{1,0:T(8,128)(2,1)}, bf16[512,2048]{1,0:T(8,128)(2,1)}, u32[]{:S(2)}, u32[]{:S(2)}) collective-permute-start(bf16[512,2048]{1,0:T(8,128)(2,1)} %get-tuple-element.214), channel_id=1, source_target_pairs={{0,2},{1,3},{4,6},{5,7},{2,0},{3,1},{6,4},{7,5}} | collective-permute-start | bytes 6291464 | tf_op jit(solution)/shard_map/ppermute | solution.py:30
  476.5 70.8 %collective-permute-start.1 = (bf16[512,2048]{1,0:T(8,128)(2,1)}, bf16[512,2048]{1,0:T(8,128)(2,1)}, u32[]{:S(2)}, u32[]{:S(2)}) collective-permute-start(bf16[512,2048]{1,0:T(8,128)(2,1)} %get-tuple-element.202), channel_id=1, source_target_pairs={{0,2},{1,3},{4,7},{5,6},{2,1},{3,0},{6,4},{7,5}} | collective-permute-start | bytes 6291464 | tf_op jit(solution)/shard_map/ppermute | solution.py:30
  478.5 126.1 %collective-permute-start.5 = (bf16[512,2048]{1,0:T(8,128)(2,1)}, bf16[512,2048]{1,0:T(8,128)(2,1)}, u32[]{:S(2)}, u32[]{:S(2)}) collective-permute-start(bf16[512,2048]{1,0:T(8,128)(2,1)} %get-tuple-element.215), channel_id=1, source_target_pairs={{0,2},{1,3},{4,6},{5,7},{2,0},{3,1},{6,4},{7,5}} | collective-permute-start | bytes 6291464 | tf_op jit(solution)/shard_map/ppermute | solution.py:30
  478.7 158.5 %collective-permute-start.6 = (bf16[512,2048]{1,0:T(8,128)(2,1)}, bf16[512,2048]{1,0:T(8,128)(2,1)}, u32[]{:S(2)}, u32[]{:S(2)}) collective-permute-start(bf16[512,2048]{1,0:T(8,128)(2,1)} %get-tuple-element.203), channel_id=1, source_target_pairs={{0,2},{1,3},{4,7},{5,6},{2,1},{3,0},{6,4},{7,5}} | collective-permute-start | bytes 6291464 | tf_op jit(solution)/shard_map/ppermute | solution.py:30
  503.3 179.8 %collective-permute-start.12 = (bf16[512,2048]{1,0:T(8,128)(2,1)}, bf16[512,2048]{1,0:T(8,128)(2,1)}, u32[]{:S(2)}, u32[]{:S(2)}) collective-permute-start(bf16[512,2048]{1,0:T(8,128)(2,1)} %get-tuple-element.216), channel_id=1, source_target_pairs={{0,2},{1,3},{4,6},{5,7},{2,0},{3,1},{6,4},{7,5}} | collective-permute-start | bytes 6291464 | tf_op jit(solution)/shard_map/ppermute | solution.py:30
  547.3 109.6 %collective-permute-start.13 = (bf16[512,2048]{1,0:T(8,128)(2,1)}, bf16[512,2048]{1,0:T(8,128)(2,1)S(1)}, u32[]{:S(2)}, u32[]{:S(2)}) collective-permute-start(bf16[512,2048]{1,0:T(8,128)(2,1)} %get-tuple-element.116), channel_id=1, source_target_pairs={{4,0},{5,1},{2,6},{3,7}} | collective-permute-start | bytes 6291464 | tf_op jit(solution)/shard_map/ppermute | solution.py:30
  563.3 95.3 %collective-permute-start.16 = (bf16[512,2048]{1,0:T(8,128)(2,1)S(1)}, bf16[512,2048]{1,0:T(8,128)(2,1)}, u32[]{:S(2)}, u32[]{:S(2)}) collective-permute-start(bf16[512,2048]{1,0:T(8,128)(2,1)S(1)} %get-tuple-element.127), channel_id=1, source_target_pairs={{4,0},{5,1},{2,6},{3,7}} | collective-permute-start | bytes 6291464 | tf_op jit(solution)/shard_map/ppermute | solution.py:30
  604.6 251.0 %collective-permute-start.20 = (bf16[512,2048]{1,0:T(8,128)(2,1)}, bf16[512,2048]{1,0:T(8,128)(2,1)}, u32[]{:S(2)}, u32[]{:S(2)}) collective-permute-start(bf16[512,2048]{1,0:T(8,128)(2,1)} %get-tuple-element.138), channel_id=1, source_target_pairs={{4,0},{5,1},{2,6},{3,7}} | collective-permute-start | bytes 6291464 | tf_op jit(solution)/shard_map/ppermute | solution.py:30
  637.2 227.9 %collective-permute-start.24 = (bf16[512,2048]{1,0:T(8,128)(2,1)}, bf16[512,2048]{1,0:T(8,128)(2,1)}, u32[]{:S(2)}, u32[]{:S(2)}) collective-permute-start(bf16[512,2048]{1,0:T(8,128)(2,1)} %get-tuple-element.150), channel_id=1, source_target_pairs={{4,0},{5,1},{2,6},{3,7}} | collective-permute-start | bytes 6291464 | tf_op jit(solution)/shard_map/ppermute | solution.py:30
  656.9 555.6 %collective-permute-start.27 = (bf16[512,2048]{1,0:T(8,128)(2,1)}, bf16[512,2048]{1,0:T(8,128)(2,1)}, u32[]{:S(2)}, u32[]{:S(2)}) collective-permute-start(bf16[512,2048]{1,0:T(8,128)(2,1)} %get-tuple-element.162), channel_id=1, source_target_pairs={{4,0},{5,1},{2,6},{3,7}} | collective-permute-start | bytes 6291464 | tf_op jit(solution)/shard_map/ppermute | solution.py:30
  658.7 68.3 %collective-permute-start.14 = (bf16[512,2048]{1,0:T(8,128)(2,1)S(1)}, bf16[512,2048]{1,0:T(8,128)(2,1)S(1)}, u32[]{:S(2)}, u32[]{:S(2)}) collective-permute-start(bf16[512,2048]{1,0:T(8,128)(2,1)S(1)} %broadcast_select_fusion.24), channel_id=1, source_target_pairs={{0,2},{1,3},{4,7},{5,6},{2,1},{3,0},{6,4},{7,5}} | collective-permute-start | bytes 6291464 | tf_op jit(solution)/shard_map/ppermute | solution.py:30
  683.1 89.8 %collective-permute-start.15 = (bf16[512,2048]{1,0:T(8,128)(2,1)S(1)}, bf16[512,2048]{1,0:T(8,128)(2,1)S(1)}, u32[]{:S(2)}, u32[]{:S(2)}) collective-permute-start(bf16[512,2048]{1,0:T(8,128)(2,1)S(1)} %copy-done.31), channel_id=1, source_target_pairs={{0,2},{1,3},{4,6},{5,7},{2,0},{3,1},{6,4},{7,5}} | collective-permute-start | bytes 6291464 | tf_op jit(solution)/shard_map/ppermute | solution.py:30
  727.0 89.9 %collective-permute-start.17 = (bf16[512,2048]{1,0:T(8,128)(2,1)S(1)}, bf16[512,2048]{1,0:T(8,128)(2,1)S(1)}, u32[]{:S(2)}, u32[]{:S(2)}) collective-permute-start(bf16[512,2048]{1,0:T(8,128)(2,1)S(1)} %broadcast_select_fusion.23), channel_id=1, source_target_pairs={{0,2},{1,3},{4,7},{5,6},{2,1},{3,0},{6,4},{7,5}} | collective-permute-start | bytes 6291464 | tf_op jit(solution)/shard_map/ppermute | solution.py:30
  772.9 448.4 %collective-permute-start.29 = (bf16[512,2048]{1,0:T(8,128)(2,1)}, bf16[512,2048]{1,0:T(8,128)(2,1)}, u32[]{:S(2)}, u32[]{:S(2)}) collective-permute-start(bf16[512,2048]{1,0:T(8,128)(2,1)} %get-tuple-element.166), channel_id=1, source_target_pairs={{4,0},{5,1},{2,6},{3,7}} | collective-permute-start | bytes 6291464 | tf_op jit(solution)/shard_map/ppermute | solution.py:30
  816.9 93.9 %collective-permute-start.43 = (f32[512,2048]{1,0:T(8,128)}, f32[512,2048]{1,0:T(8,128)}, u32[]{:S(2)}, u32[]{:S(2)}) collective-permute-start(f32[512,2048]{1,0:T(8,128)} %slice_add_fusion.14), channel_id=1, source_target_pairs={{0,4},{1,5},{6,2},{7,3}} | collective-permute-start | bytes 12582920 | tf_op jit(solution)/shard_map/ppermute | solution.py:30
  855.6 144.0 %collective-permute-start.44 = (f32[512,2048]{1,0:T(8,128)}, f32[512,2048]{1,0:T(8,128)}, u32[]{:S(2)}, u32[]{:S(2)}) collective-permute-start(f32[512,2048]{1,0:T(8,128)} %slice_add_fusion.12), channel_id=1, source_target_pairs={{0,4},{1,5},{6,2},{7,3}} | collective-permute-start | bytes 12582920 | tf_op jit(solution)/shard_map/ppermute | solution.py:30
  865.1 139.8 %collective-permute-start.18 = (bf16[512,4096]{1,0:T(8,128)(2,1)}, bf16[512,4096]{1,0:T(8,128)(2,1)}, u32[]{:S(2)}, u32[]{:S(2)}) collective-permute-start(bf16[512,4096]{1,0:T(8,128)(2,1)} %pad_maximum_fusion), channel_id=1, source_target_pairs={{0,1},{1,0},{4,5},{5,4},{2,3},{3,2},{6,7},{7,6}} | collective-permute-start | bytes 12582920 | tf_op jit(solution)/shard_map/ppermute | solution.py:30
  910.8 317.4 %collective-permute-start.32 = (bf16[512,2048]{1,0:T(8,128)(2,1)}, bf16[512,2048]{1,0:T(8,128)(2,1)}, u32[]{:S(2)}, u32[]{:S(2)}) collective-permute-start(bf16[512,2048]{1,0:T(8,128)(2,1)} %get-tuple-element.172), channel_id=1, source_target_pairs={{4,0},{5,1},{2,6},{3,7}} | collective-permute-start | bytes 6291464 | tf_op jit(solution)/shard_map/ppermute | solution.py:30
  999.6 49.0 %collective-permute-start.19 = (bf16[512,2048]{1,0:T(8,128)(2,1)S(1)}, bf16[512,2048]{1,0:T(8,128)(2,1)S(1)}, u32[]{:S(2)}, u32[]{:S(2)}) collective-permute-start(bf16[512,2048]{1,0:T(8,128)(2,1)S(1)} %copy-done.30), channel_id=1, source_target_pairs={{0,2},{1,3},{4,6},{5,7},{2,0},{3,1},{6,4},{7,5}} | collective-permute-start | bytes 6291464 | tf_op jit(solution)/shard_map/ppermute | solution.py:30
  1004.9 86.3 %collective-permute-start.21 = (bf16[512,2048]{1,0:T(8,128)(2,1)S(1)}, bf16[512,2048]{1,0:T(8,128)(2,1)S(1)}, u32[]{:S(2)}, u32[]{:S(2)}) collective-permute-start(bf16[512,2048]{1,0:T(8,128)(2,1)S(1)} %copy-done.34), channel_id=1, source_target_pairs={{0,2},{1,3},{4,7},{5,6},{2,1},{3,0},{6,4},{7,5}} | collective-permute-start | bytes 6291464 | tf_op jit(solution)/shard_map/ppermute | solution.py:30
  1048.6 88.3 %collective-permute-start.22 = (bf16[512,4096]{1,0:T(8,128)(2,1)S(1)}, bf16[512,4096]{1,0:T(8,128)(2,1)}, u32[]{:S(2)}, u32[]{:S(2)}) collective-permute-start(bf16[512,4096]{1,0:T(8,128)(2,1)S(1)} %pad_maximum_fusion.1), channel_id=1, source_target_pairs={{0,1},{1,0},{4,5},{5,4},{2,3},{3,2},{6,7},{7,6}} | collective-permute-start | bytes 12582920 | tf_op jit(solution)/shard_map/ppermute | solution.py:30
  1091.2 60.5 %collective-permute-start.23 = (bf16[512,2048]{1,0:T(8,128)(2,1)S(1)}, bf16[512,2048]{1,0:T(8,128)(2,1)S(1)}, u32[]{:S(2)}, u32[]{:S(2)}) collective-permute-start(bf16[512,2048]{1,0:T(8,128)(2,1)S(1)} %copy-done.29), channel_id=1, source_target_pairs={{0,2},{1,3},{4,6},{5,7},{2,0},{3,1},{6,4},{7,5}} | collective-permute-start | bytes 6291464 | tf_op jit(solution)/shard_map/ppermute | solution.py:30
  1136.9 47.3 %collective-permute-start.25 = (bf16[512,2048]{1,0:T(8,128)(2,1)S(1)}, bf16[512,2048]{1,0:T(8,128)(2,1)S(1)}, u32[]{:S(2)}, u32[]{:S(2)}) collective-permute-start(bf16[512,2048]{1,0:T(8,128)(2,1)S(1)} %copy-done.32), channel_id=1, source_target_pairs={{0,2},{1,3},{4,7},{5,6},{2,1},{3,0},{6,4},{7,5}} | collective-permute-start | bytes 6291464 | tf_op jit(solution)/shard_map/ppermute | solution.py:30
  1151.7 83.1 %collective-permute-start.34 = (bf16[512,2048]{1,0:T(8,128)(2,1)S(1)}, bf16[512,2048]{1,0:T(8,128)(2,1)S(1)}, u32[]{:S(2)}, u32[]{:S(2)}) collective-permute-start(bf16[512,2048]{1,0:T(8,128)(2,1)S(1)} %copy-done), channel_id=1, source_target_pairs={{4,0},{5,1},{2,6},{3,7}} | collective-permute-start | bytes 6291464 | tf_op jit(solution)/shard_map/ppermute | solution.py:30
  1184.2 93.4 %collective-permute-start.45 = (f32[512,2048]{1,0:T(8,128)}, f32[512,2048]{1,0:T(8,128)}, u32[]{:S(2)}, u32[]{:S(2)}) collective-permute-start(f32[512,2048]{1,0:T(8,128)} %slice_add_fusion.10), channel_id=1, source_target_pairs={{0,4},{1,5},{6,2},{7,3}} | collective-permute-start | bytes 12582920 | tf_op jit(solution)/shard_map/ppermute | solution.py:30
  1212.5 155.0 %collective-permute-start.46 = (f32[512,2048]{1,0:T(8,128)}, f32[512,2048]{1,0:T(8,128)}, u32[]{:S(2)}, u32[]{:S(2)}) collective-permute-start(f32[512,2048]{1,0:T(8,128)} %slice_add_fusion.8), channel_id=1, source_target_pairs={{0,4},{1,5},{6,2},{7,3}} | collective-permute-start | bytes 12582920 | tf_op jit(solution)/shard_map/ppermute | solution.py:30
  1221.2 457.1 %collective-permute-start.40 = (f32[512,2048]{1,0:T(8,128)}, f32[512,2048]{1,0:T(8,128)}, u32[]{:S(2)}, u32[]{:S(2)}) collective-permute-start(f32[512,2048]{1,0:T(8,128)} %slice_add_fusion.4), channel_id=1, source_target_pairs={{0,4},{1,5},{6,2},{7,3}} | collective-permute-start | bytes 12582920 | tf_op jit(solution)/shard_map/ppermute | solution.py:30
  1228.2 330.6 %collective-permute-start.47 = (f32[512,2048]{1,0:T(8,128)}, f32[512,2048]{1,0:T(8,128)}, u32[]{:S(2)}, u32[]{:S(2)}) collective-permute-start(f32[512,2048]{1,0:T(8,128)} %slice_add_fusion.6), channel_id=1, source_target_pairs={{0,4},{1,5},{6,2},{7,3}} | collective-permute-start | bytes 12582920 | tf_op jit(solution)/shard_map/ppermute | solution.py:30
  1234.8 152.5 %collective-permute-start.26 = (bf16[512,4096]{1,0:T(8,128)(2,1)}, bf16[512,4096]{1,0:T(8,128)(2,1)}, u32[]{:S(2)}, u32[]{:S(2)}) collective-permute-start(bf16[512,4096]{1,0:T(8,128)(2,1)} %pad_maximum_fusion.2), channel_id=1, source_target_pairs={{0,1},{1,0},{4,5},{5,4},{2,3},{3,2},{6,7},{7,6}} | collective-permute-start | bytes 12582920 | tf_op jit(solution)/shard_map/ppermute | solution.py:30
  1277.6 124.6 %collective-permute-start.28 = (bf16[512,2048]{1,0:T(8,128)(2,1)}, bf16[512,2048]{1,0:T(8,128)(2,1)S(1)}, u32[]{:S(2)}, u32[]{:S(2)}) collective-permute-start(bf16[512,2048]{1,0:T(8,128)(2,1)} %broadcast_select_fusion.14), channel_id=1, source_target_pairs={{0,2},{1,3},{4,6},{5,7},{2,0},{3,1},{6,4},{7,5}} | collective-permute-start | bytes 6291464 | tf_op jit(solution)/shard_map/ppermute | solution.py:30
  1367.5 48.8 %collective-permute-start.30 = (bf16[512,2048]{1,0:T(8,128)(2,1)}, bf16[512,2048]{1,0:T(8,128)(2,1)S(1)}, u32[]{:S(2)}, u32[]{:S(2)}) collective-permute-start(bf16[512,2048]{1,0:T(8,128)(2,1)} %broadcast_select_fusion.13), channel_id=1, source_target_pairs={{0,2},{1,3},{4,7},{5,6},{2,1},{3,0},{6,4},{7,5}} | collective-permute-start | bytes 6291464 | tf_op jit(solution)/shard_map/ppermute | solution.py:30
  1387.3 77.5 %collective-permute-start.31 = (bf16[512,4096]{1,0:T(8,128)(2,1)S(1)}, bf16[512,4096]{1,0:T(8,128)(2,1)}, u32[]{:S(2)}, u32[]{:S(2)}) collective-permute-start(bf16[512,4096]{1,0:T(8,128)(2,1)S(1)} %pad_maximum_fusion.3), channel_id=1, source_target_pairs={{0,1},{1,0},{4,5},{5,4},{2,3},{3,2},{6,7},{7,6}} | collective-permute-start | bytes 12582920 | tf_op jit(solution)/shard_map/ppermute | solution.py:30
  1402.3 81.2 %collective-permute-start.33 = (bf16[512,2048]{1,0:T(8,128)(2,1)S(1)}, bf16[512,2048]{1,0:T(8,128)(2,1)S(1)}, u32[]{:S(2)}, u32[]{:S(2)}) collective-permute-start(bf16[512,2048]{1,0:T(8,128)(2,1)S(1)} %copy-done.33), channel_id=1, source_target_pairs={{0,2},{1,3},{4,6},{5,7},{2,0},{3,1},{6,4},{7,5}} | collective-permute-start | bytes 6291464 | tf_op jit(solution)/shard_map/ppermute | solution.py:30
  1416.4 88.1 %collective-permute-start.35 = (bf16[512,2048]{1,0:T(8,128)(2,1)}, bf16[512,2048]{1,0:T(8,128)(2,1)S(1)}, u32[]{:S(2)}, u32[]{:S(2)}) collective-permute-start(bf16[512,2048]{1,0:T(8,128)(2,1)} %broadcast_select_fusion.9), channel_id=1, source_target_pairs={{0,2},{1,3},{4,7},{5,6},{2,1},{3,0},{6,4},{7,5}} | collective-permute-start | bytes 6291464 | tf_op jit(solution)/shard_map/ppermute | solution.py:30
  1464.8 213.5 %collective-permute-start.41 = (f32[512,2048]{1,0:T(8,128)}, f32[512,2048]{1,0:T(8,128)}, u32[]{:S(2)}, u32[]{:S(2)}) collective-permute-start(f32[512,2048]{1,0:T(8,128)} %slice_add_fusion.2), channel_id=1, source_target_pairs={{0,4},{1,5},{6,2},{7,3}} | collective-permute-start | bytes 12582920 | tf_op jit(solution)/shard_map/ppermute | solution.py:30
  1520.9 204.6 %collective-permute-start.42 = (f32[512,2048]{1,0:T(8,128)}, f32[512,2048]{1,0:T(8,128)}, u32[]{:S(2)}, u32[]{:S(2)}) collective-permute-start(f32[512,2048]{1,0:T(8,128)} %slice_add_fusion.1), channel_id=1, source_target_pairs={{0,4},{1,5},{6,2},{7,3}} | collective-permute-start | bytes 12582920 | tf_op jit(solution)/shard_map/ppermute | solution.py:30
  1531.4 48.1 %collective-permute-start.36 = (bf16[512,4096]{1,0:T(8,128)(2,1)}, bf16[512,4096]{1,0:T(8,128)(2,1)}, u32[]{:S(2)}, u32[]{:S(2)}) collective-permute-start(bf16[512,4096]{1,0:T(8,128)(2,1)} %pad_maximum_fusion.4), channel_id=1, source_target_pairs={{0,1},{1,0},{4,5},{5,4},{2,3},{3,2},{6,7},{7,6}} | collective-permute-start | bytes 12582920 | tf_op jit(solution)/shard_map/ppermute | solution.py:30
  1558.8 49.2 %collective-permute-start.37 = (bf16[512,4096]{1,0:T(8,128)(2,1)}, bf16[512,4096]{1,0:T(8,128)(2,1)}, u32[]{:S(2)}, u32[]{:S(2)}) collective-permute-start(bf16[512,4096]{1,0:T(8,128)(2,1)} %pad_maximum_fusion.5), channel_id=1, source_target_pairs={{0,1},{1,0},{4,5},{5,4},{2,3},{3,2},{6,7},{7,6}} | collective-permute-start | bytes 12582920 | tf_op jit(solution)/shard_map/ppermute | solution.py:30
  1579.6 56.7 %collective-permute-start.38 = (bf16[512,4096]{1,0:T(8,128)(2,1)}, bf16[512,4096]{1,0:T(8,128)(2,1)}, u32[]{:S(2)}, u32[]{:S(2)}) collective-permute-start(bf16[512,4096]{1,0:T(8,128)(2,1)} %pad_maximum_fusion.6), channel_id=1, source_target_pairs={{0,1},{1,0},{4,5},{5,4},{2,3},{3,2},{6,7},{7,6}} | collective-permute-start | bytes 12582920 | tf_op jit(solution)/shard_map/ppermute | solution.py:30
  1608.0 56.5 %collective-permute-start.39 = (bf16[512,4096]{1,0:T(8,128)(2,1)}, bf16[512,4096]{1,0:T(8,128)(2,1)S(1)}, u32[]{:S(2)}, u32[]{:S(2)}) collective-permute-start(bf16[512,4096]{1,0:T(8,128)(2,1)} %pad_maximum_fusion.7), channel_id=1, source_target_pairs={{0,1},{1,0},{4,5},{5,4},{2,3},{3,2},{6,7},{7,6}} | collective-permute-start | bytes 12582920 | tf_op jit(solution)/shard_map/ppermute | solution.py:30
  (40 other events, 1090.1 us)
